TPU v7x, 8 devices: a whole 2x2x1 slice. The times are simulated.
8 devices in a mesh: hp: 1 (over z), cp: 8 (over y, x, core).
Axes of the slice: x: 2, y: 2, z: 1, core: 2. Of those that a mesh axis runs over, the one named last changes fastest.
Arguments:
- q_heads: bfloat16 [2048, 16, 256], P('cp', 'hp')
- k_heads: bfloat16 [2048, 16, 256], P('cp', 'hp')
- v_heads: bfloat16 [2048, 16, 256], P('cp', 'hp')
- o_heads: bfloat16 [2048, 16, 256], P('cp', 'hp')
- do_heads: bfloat16 [2048, 16, 256], P('cp', 'hp')
- lse_rows: float32 [2048, 16], P('cp', 'hp')
- cu_seqlens: int32 [67], replicated
Outputs:
- output 1: bfloat16 [2048, 16, 256], P('cp', 'hp')
- output 2: bfloat16 [2048, 16, 256], P('cp', 'hp')
- output 3: bfloat16 [2048, 16, 256], P('cp', 'hp')
All inputs are finite; a program needn't handle non-finite values.
Results may differ from a plain program's by a relative error of at most 0.001.
Values are sent between devices in bfloat16 or wider.
A program may use at most 1 GiB of HBM per device.

v0:
```python
import functools

import jax
import jax.numpy as jnp
from jax import lax
from jax.experimental import pallas as pl
from jax.experimental.pallas import tpu as pltpu
from jax.sharding import PartitionSpec as P

REACH = 3
TILE_HEADS = 8
ROW_PARTS = 2
LOG2E = 1.4426950408889634
MESH_ID = pl.DeviceIdType.MESH


def to_dev(idx):
    return {"cp": idx}


def greet_all(n_dev, me):
    barrier = pltpu.get_barrier_semaphore()
    for step in range(1, n_dev):
        pl.semaphore_signal(barrier, inc=1, device_id=to_dev(lax.rem(me + step, n_dev)), device_id_type=MESH_ID)
    pl.semaphore_wait(barrier, n_dev - 1)


def stat_copies(me, n_dev, stat_ref, swin_ref, send_sem, recv_sem):
    out = []
    for dist in range(1, REACH + 1):
        copy = pltpu.make_async_remote_copy(src_ref=stat_ref, dst_ref=swin_ref.at[dist - 1], send_sem=send_sem.at[dist - 1], recv_sem=recv_sem.at[dist - 1], device_id=to_dev(lax.rem(me + n_dev - dist, n_dev)), device_id_type=MESH_ID)
        out.append((dist, copy))
    return out


def far_kernel(n_dev, kv_ref, qd_ref, stat_ref, win_ref, swin_ref, st_s, st_r, kv_s, kv_r, qd_s, qd_r):
    me = lax.axis_index("cp")
    greet_all(n_dev, me)
    stats = stat_copies(me, n_dev, stat_ref, swin_ref, st_s, st_r)
    for dist, copy in stats:
        up = pltpu.make_async_remote_copy(src_ref=kv_ref, dst_ref=win_ref.at[dist - 1], send_sem=kv_s.at[dist - 1], recv_sem=kv_r.at[dist - 1], device_id=to_dev(lax.rem(me + dist, n_dev)), device_id_type=MESH_ID)
        down = pltpu.make_async_remote_copy(src_ref=qd_ref, dst_ref=win_ref.at[REACH + dist - 1], send_sem=qd_s.at[dist - 1], recv_sem=qd_r.at[dist - 1], device_id=to_dev(lax.rem(me + n_dev - dist, n_dev)), device_id_type=MESH_ID)
        pl.when(me + dist < n_dev)(up.start)
        pl.when(me >= dist)(down.start)
        pl.when(me >= dist)(copy.start)
    for dist, copy in stats:
        up = pltpu.make_async_remote_copy(src_ref=kv_ref, dst_ref=win_ref.at[dist - 1], send_sem=kv_s.at[dist - 1], recv_sem=kv_r.at[dist - 1], device_id=to_dev(lax.rem(me + dist, n_dev)), device_id_type=MESH_ID)
        down = pltpu.make_async_remote_copy(src_ref=qd_ref, dst_ref=win_ref.at[REACH + dist - 1], send_sem=qd_s.at[dist - 1], recv_sem=qd_r.at[dist - 1], device_id=to_dev(lax.rem(me + n_dev - dist, n_dev)), device_id_type=MESH_ID)
        pl.when(me + dist < n_dev)(up.wait_send)
        pl.when(me >= dist)(up.wait_recv)
        pl.when(me >= dist)(down.wait_send)
        pl.when(me + dist < n_dev)(down.wait_recv)
        pl.when(me >= dist)(copy.wait_send)
        pl.when(me + dist < n_dev)(copy.wait_recv)


def nt_dot(a, b):
    return lax.dot_general(a, b, (((1,), (1,)), ((), ())), preferred_element_type=jnp.float32)


def nn_dot(a, b):
    return lax.dot_general(a, b, (((1,), (0,)), ((), ())), preferred_element_type=jnp.float32)


def tn_dot(a, b):
    return lax.dot_general(a, b, (((0,), (0,)), ((), ())), preferred_element_type=jnp.float32)


def block_terms(score_scale, k_blk, v_blk, q_blk, do_blk, lse_row, delta_row, start_row, k_base, q_base):
    s_t = nt_dot(k_blk, q_blk)
    dp_t = nt_dot(v_blk, do_blk)
    k_pos = k_base + lax.broadcasted_iota(jnp.int32, s_t.shape, 0)
    q_pos = q_base + lax.broadcasted_iota(jnp.int32, s_t.shape, 1)
    keep = (k_pos >= start_row) & (k_pos <= q_pos)
    p_t = jnp.where(keep, jnp.exp2(s_t * (score_scale * LOG2E) - lse_row * LOG2E), 0.0)
    ds_t = (p_t * (dp_t - delta_row)).astype(jnp.bfloat16)
    return p_t.astype(jnp.bfloat16), ds_t


def grad_kernel(score_scale, flag_ref, qd_ref, kv_ref, win_ref, stat_ref, swin_ref, start_ref, dq_ref, dk_ref, dv_ref, dq_acc, dk_acc, dv_acc):
    head = pl.program_id(0)
    n_heads = pl.num_programs(0)
    base = flag_ref[2 * REACH]
    n_tok = qd_ref.shape[2]

    terms = functools.partial(block_terms, score_scale)

    q_blk, do_blk = qd_ref[0, 0], qd_ref[1, 0]
    k_blk, v_blk = kv_ref[0, 0], kv_ref[1, 0]
    lse_own, delta_own = stat_ref[pl.ds(head, 1), :], stat_ref[pl.ds(n_heads + head, 1), :]
    p_t, ds_t = terms(k_blk, v_blk, q_blk, do_blk, lse_own, delta_own, start_ref[0:1, :], base, base)
    dv_acc[...] = nn_dot(p_t, do_blk)
    dk_acc[...] = nn_dot(ds_t, q_blk)
    dq_acc[...] = tn_dot(ds_t, k_blk)
    for dist in range(1, REACH + 1):
        @pl.when(flag_ref[dist - 1] == 1)
        def _():
            k_far, v_far = win_ref[dist - 1, 0, 0], win_ref[dist - 1, 1, 0]
            _, ds_far = terms(k_far, v_far, q_blk, do_blk, lse_own, delta_own, start_ref[0:1, :], base - dist * n_tok, base)
            dq_acc[...] += tn_dot(ds_far, k_far)

        @pl.when(flag_ref[REACH + dist - 1] == 1)
        def _():
            q_far, do_far = win_ref[REACH + dist - 1, 0, 0], win_ref[REACH + dist - 1, 1, 0]
            lse_far = swin_ref[dist - 1, pl.ds(head, 1), :]
            delta_far = swin_ref[dist - 1, pl.ds(n_heads + head, 1), :]
            p_far, ds_far = terms(k_blk, v_blk, q_far, do_far, lse_far, delta_far, start_ref[dist:dist + 1, :], base, base + dist * n_tok)
            dv_acc[...] += nn_dot(p_far, do_far)
            dk_acc[...] += nn_dot(ds_far, q_far)

    dq_ref[0] = (dq_acc[...] * score_scale).astype(dq_ref.dtype)
    dk_ref[0] = (dk_acc[...] * score_scale).astype(dk_ref.dtype)
    dv_ref[0] = dv_acc[...].astype(dv_ref.dtype)


def near_kernel(n_dev, score_scale, cu_ref, q_ref, k_ref, v_ref, o_ref, do_ref, lse_ref, dq_ref, dk_ref, dv_ref,
                raw, raw_o, qd, kv, pk, win, stat, swin, starts, out_hm, dq_acc, dk_acc, dv_acc,
                ld_sem, o_sem, out_sem, st_s, st_r, own_s, own_r, x_s, x_r, y_s, y_r, fx_s, fx_r, fy_s, fy_r):
    me = lax.axis_index("cp")
    core = lax.rem(me, 2)
    chip = me // 2
    chip_odd = lax.rem(chip, 2)
    n_tok, n_heads, _ = q_ref.shape
    part = n_tok // ROW_PARTS
    base = me * n_tok
    first_chip, last_chip = chip == 0, chip == n_dev // 2 - 1
    not_first, not_last = jnp.logical_not(first_chip), jnp.logical_not(last_chip)
    relays = first_chip | last_chip
    middle = jnp.logical_not(relays)
    x_dev, y_dev, mate = me + 2 - 4 * chip_odd, lax.rem(me + 4, n_dev), me + 1 - 2 * core
    x_dst = 1 + 2 * chip_odd
    x_slot = 3 - 2 * chip_odd
    y_slot = 4 - x_slot

    def remote(src, dst, s_sem, r_sem, dev):
        return pltpu.make_async_remote_copy(src_ref=src, dst_ref=dst, send_sem=s_sem, recv_sem=r_sem, device_id=to_dev(dev), device_id_type=MESH_ID)

    def block(slot, h, r):
        return win.at[slot, :, h, pl.ds(r * part, part)]

    def x_copy(h, r):
        return remote(pk.at[:, h, pl.ds(r * part, part)], block(x_dst, h, r), x_s.at[h, r], x_r.at[h, r], x_dev)

    def y_copy(h, r):
        return remote(block(x_slot, h, r), block(y_slot, h, r), y_s.at[h, r], y_r.at[h, r], y_dev)

    def fx_copy(h, r):
        return remote(block(x_slot, h, r), block(4 - 2 * core - 2 * chip_odd, h, r), fx_s.at[h, r], fx_r.at[h, r], mate)

    def fy_copy(h, r):
        return remote(block(y_slot, h, r), block(2 - 2 * core + 2 * chip_odd, h, r), fy_s.at[h, r], fy_r.at[h, r], mate)

    def own_kv(h):
        return remote(kv.at[:, h], win.at[0, :, h], own_s.at[h], own_r.at[h], mate)

    def own_qd(h):
        return remote(qd.at[:, h], win.at[4, :, h], own_s.at[h], own_r.at[h], mate)

    def load(half, which):
        src = (q_ref, k_ref, do_ref, v_ref)[which]
        return pltpu.make_async_copy(src.at[:, pl.ds(half * TILE_HEADS, TILE_HEADS)], raw.at[half, which], ld_sem.at[half, which])

    halves = n_heads // TILE_HEADS
    for half in range(halves):
        for which in range(4):
            load(half, which).start()
    load_o = pltpu.make_async_copy(o_ref, raw_o, o_sem)
    load_o.start()

    chip_pos = chip * 2 * n_tok
    pos = base + n_tok * lax.broadcasted_iota(jnp.int32, starts.shape, 0) + lax.broadcasted_iota(jnp.int32, starts.shape, 1)

    def scan_docs(n, carry):
        found, cross_end = carry
        first, last = cu_ref[n], cu_ref[n + 1]
        crosses = (first < chip_pos) & (last > chip_pos)
        return jnp.where(first <= pos, jnp.maximum(found, first), found), jnp.where(crosses, last, cross_end)

    found, cross_end = lax.fori_loop(0, cu_ref.shape[0] - 1, scan_docs, (jnp.zeros(starts.shape, jnp.int32), 0))
    starts[...] = jnp.where(pos < n_dev * n_tok, found, n_dev * n_tok)
    send_rows = jnp.clip(cross_end - base, 0, n_tok)
    send_qd = lax.broadcasted_iota(jnp.int32, (TILE_HEADS, n_tok, q_ref.shape[2]), 1) < send_rows

    greet_all(n_dev, me)
    stats = stat_copies(me, n_dev, stat, swin, st_s, st_r)

    def send_heads(half):
        for h in range(half * TILE_HEADS, (half + 1) * TILE_HEADS):
            for r in range(ROW_PARTS):
                x_copy(h, r).start()
        for h in range(half * TILE_HEADS, (half + 1) * TILE_HEADS):
            pl.when(core == 0)(own_kv(h).start)
            pl.when(core == 1)(own_qd(h).start)

    for half in range(halves):
        rows = pl.ds(half * TILE_HEADS, TILE_HEADS)
        for pair in range(2):
            load(half, 2 * pair).wait()
            load(half, 2 * pair + 1).wait()
            q_side = jnp.swapaxes(raw[half, 2 * pair], 0, 1)
            k_side = jnp.swapaxes(raw[half, 2 * pair + 1], 0, 1)
            pk[pair, rows] = jnp.where(send_qd, q_side, k_side)
            qd[pair, rows] = q_side
            kv[pair, rows] = k_side
        if half == 0:
            load_o.wait()
            stat[0:n_heads, :] = lse_ref[...]
        delta = jnp.sum(raw[half, 2].astype(jnp.float32) * raw_o[:, half * TILE_HEADS:(half + 1) * TILE_HEADS, :].astype(jnp.float32), axis=-1)
        stat[n_heads + half * TILE_HEADS:n_heads + (half + 1) * TILE_HEADS, :] = delta.T
        send_heads(half)
    for dist, copy in stats:
        pl.when(me >= dist)(copy.start)
    for dist, copy in stats:
        pl.when(me + dist < n_dev)(copy.wait_recv)

    terms = functools.partial(block_terms, score_scale)

    def arrive(h):
        for r in range(ROW_PARTS):
            x_copy(h, r).wait_recv()
            pl.when(relays)(lambda: y_copy(h, r).start())
            fx_copy(h, r).start()

    def arrive_y(h):
        for r in range(ROW_PARTS):
            y_copy(h, r).wait_recv()
            fy_copy(h, r).start()

    def compute(h):
        own_qd(h).wait_recv()
        for r in range(ROW_PARTS):
            fx_copy(h, r).wait_recv()

        @pl.when(middle)
        def _():
            for r in range(ROW_PARTS):
                fy_copy(h, r).wait_recv()

        q_blk, do_blk, k_blk, v_blk = qd[0, h], qd[1, h], kv[0, h], kv[1, h]
        lse_own, delta_own = stat[pl.ds(h, 1), :], stat[pl.ds(n_heads + h, 1), :]
        p_t, ds_t = terms(k_blk, v_blk, q_blk, do_blk, lse_own, delta_own, starts[0:1, :], base, base)
        dv_acc[...] = nn_dot(p_t, do_blk)
        dk_acc[...] = nn_dot(ds_t, q_blk)
        dq_acc[...] = tn_dot(ds_t, k_blk)
        for dist in range(1, REACH + 1):
            k_here = {1: (core == 1) | not_first, 2: not_first, 3: (core == 1) & not_first}[dist]
            q_here = {1: (core == 0) | not_last, 2: not_last, 3: (core == 0) & not_last}[dist]

            @pl.when(k_here)
            def _():
                k_far, v_far = win[dist - 1, 0, h], win[dist - 1, 1, h]
                _, ds_far = terms(k_far, v_far, q_blk, do_blk, lse_own, delta_own, starts[0:1, :], base - dist * n_tok, base)
                dq_acc[...] += tn_dot(ds_far, k_far)

            @pl.when(q_here)
            def _():
                q_far, do_far = win[5 - dist, 0, h], win[5 - dist, 1, h]
                lse_far = swin[dist - 1, pl.ds(h, 1), :]
                delta_far = swin[dist - 1, pl.ds(n_heads + h, 1), :]
                p_far, ds_far = terms(k_blk, v_blk, q_far, do_far, lse_far, delta_far, starts[dist:dist + 1, :], base, base + dist * n_tok)
                dv_acc[...] += nn_dot(p_far, do_far)
                dk_acc[...] += nn_dot(ds_far, q_far)

        h_in = lax.rem(h, TILE_HEADS)
        out_hm[0, h_in] = (dq_acc[...] * score_scale).astype(out_hm.dtype)
        out_hm[1, h_in] = (dk_acc[...] * score_scale).astype(out_hm.dtype)
        out_hm[2, h_in] = dv_acc[...].astype(out_hm.dtype)

    def out_copy(half, which):
        dst = (dq_ref, dk_ref, dv_ref)[which]
        rows = pl.ds(half * TILE_HEADS, TILE_HEADS)
        return pltpu.make_async_copy(raw.at[half, which], dst.at[:, rows], out_sem.at[half, which])

    def step(t, carry):
        pl.when(t < n_heads)(lambda: arrive(t))
        pl.when(t >= 2)(lambda: compute(t - 2))
        for half in range(halves):
            @pl.when(t - 2 == (half + 1) * TILE_HEADS - 1)
            def _():
                for which in range(3):
                    raw[half, which] = jnp.swapaxes(out_hm[which], 0, 1)
                for which in range(3):
                    out_copy(half, which).start()
        pl.when((t >= 1) & (t <= n_heads) & middle)(lambda: arrive_y(t - 1))
        return carry

    lax.fori_loop(0, n_heads + 2, step, 0)

    def drain(h, carry):
        own_kv(h).wait_send()
        for r in range(ROW_PARTS):
            x_copy(h, r).wait_send()
            fx_copy(h, r).wait_send()
            pl.when(relays)(lambda: y_copy(h, r).wait_send())
            pl.when(middle)(lambda: fy_copy(h, r).wait_send())
        return carry

    lax.fori_loop(0, n_heads, drain, 0)
    for dist, copy in stats:
        pl.when(me >= dist)(copy.wait_send)
    for half in range(halves):
        for which in range(3):
            out_copy(half, which).wait()


def solution(mesh):
    n_dev = mesh.shape["cp"]
    head_spec = P("cp", "hp", None)
    row_spec = P("cp", "hp")
    any_spec = pl.BlockSpec(memory_space=pl.ANY)
    vmem_spec = pl.BlockSpec(memory_space=pltpu.VMEM)
    smem_spec = pl.BlockSpec(memory_space=pltpu.SMEM)
    dma = pltpu.SemaphoreType.DMA

    def device_fn(q_loc, k_loc, v_loc, o_loc, do_loc, lse_loc, cu_seqlens):
        n_tok, n_heads, head_dim = q_loc.shape
        seq_len = n_tok * n_dev
        score_scale = head_dim ** -0.5
        me = lax.axis_index("cp")
        pair_shape = (2, n_heads, n_tok, head_dim)

        def wide(q_loc, k_loc, v_loc, o_loc, do_loc, lse_loc, cu_seqlens):
            def doc_start(pos):
                found = jnp.max(jnp.where(cu_seqlens <= pos[..., None], cu_seqlens, 0), axis=-1)
                return jnp.where(pos < seq_len, found, seq_len).astype(jnp.int32)

            base = me * n_tok
            start_rows = doc_start(base + jnp.arange((REACH + 1) * n_tok, dtype=jnp.int32)).reshape(REACH + 1, n_tok)
            dists = jnp.arange(1, REACH + 1, dtype=jnp.int32)
            kv_on = start_rows[0, 0] < base - (dists - 1) * n_tok
            qd_on = start_rows[1:, 0] < base + n_tok
            flags = jnp.concatenate([kv_on.astype(jnp.int32), qd_on.astype(jnp.int32), base[None]]).astype(jnp.int32)
            delta_loc = jnp.einsum("shd,shd->sh", do_loc, o_loc, preferred_element_type=jnp.float32)
            stat = jnp.concatenate([lse_loc.T, delta_loc.T])
            qd = jnp.stack([q_loc, do_loc]).transpose(0, 2, 1, 3)
            kv = jnp.stack([k_loc, v_loc]).transpose(0, 2, 1, 3)
            win_shapes = (jax.ShapeDtypeStruct((2 * REACH,) + qd.shape, qd.dtype), jax.ShapeDtypeStruct((REACH,) + stat.shape, stat.dtype))
            win, swin = pl.pallas_call(functools.partial(far_kernel, n_dev), out_shape=win_shapes, in_specs=[any_spec] * 3, out_specs=(any_spec, any_spec),
                                       scratch_shapes=[dma((REACH,))] * 6,
                                       compiler_params=pltpu.CompilerParams(collective_id=1, has_side_effects=True), name="wide_exchange")(kv, qd, stat)
            head_blk = lambda h, flag: (0, h, 0, 0)
            full2 = lambda h, flag: (0, 0)
            out_blk = pl.BlockSpec((1, n_tok, head_dim), lambda h, flag: (h, 0, 0))
            out_one = jax.ShapeDtypeStruct((n_heads, n_tok, head_dim), jnp.bfloat16)
            dq, dk, dv = pl.pallas_call(
                functools.partial(grad_kernel, score_scale),
                grid_spec=pltpu.PrefetchScalarGridSpec(
                    num_scalar_prefetch=1, grid=(n_heads,),
                    in_specs=[pl.BlockSpec((2, 1, n_tok, head_dim), head_blk), pl.BlockSpec((2, 1, n_tok, head_dim), head_blk),
                              pl.BlockSpec((2 * REACH, 2, 1, n_tok, head_dim), lambda h, flag: (0, 0, h, 0, 0)),
                              pl.BlockSpec(stat.shape, full2), pl.BlockSpec((REACH,) + stat.shape, lambda h, flag: (0, 0, 0)),
                              pl.BlockSpec((REACH + 1, n_tok), full2)],
                    out_specs=[out_blk] * 3,
                    scratch_shapes=[pltpu.VMEM((n_tok, head_dim), jnp.float32)] * 3),
                out_shape=(out_one, out_one, out_one), name="grads",
            )(flags, qd, kv, win, stat, swin, start_rows)
            return tuple(item.transpose(1, 0, 2) for item in (dq, dk, dv))

        def near(q_loc, k_loc, v_loc, o_loc, do_loc, lse_loc, cu_seqlens):
            out_one = jax.ShapeDtypeStruct(q_loc.shape, q_loc.dtype)
            bf16, f32 = jnp.bfloat16, jnp.float32
            return pl.pallas_call(
                functools.partial(near_kernel, n_dev, score_scale),
                out_shape=(out_one, out_one, out_one),
                in_specs=[smem_spec] + [any_spec] * 5 + [vmem_spec], out_specs=(any_spec,) * 3,
                scratch_shapes=[pltpu.VMEM((n_heads // TILE_HEADS, 4, n_tok, TILE_HEADS, head_dim), bf16), pltpu.VMEM(q_loc.shape, bf16)]
                + [pltpu.VMEM(pair_shape, bf16)] * 3 + [pltpu.VMEM((5,) + pair_shape, bf16)]
                + [pltpu.VMEM((2 * n_heads, n_tok), f32), pltpu.VMEM((REACH, 2 * n_heads, n_tok), f32), pltpu.VMEM((8, n_tok), jnp.int32)]
                + [pltpu.VMEM((3, TILE_HEADS, n_tok, head_dim), bf16)] + [pltpu.VMEM((n_tok, head_dim), f32)] * 3
                + [dma((n_heads // TILE_HEADS, 4)), dma, dma((n_heads // TILE_HEADS, 3)), dma((REACH,)), dma((REACH,)), dma((n_heads,)), dma((n_heads,))]
                + [dma((n_heads, ROW_PARTS))] * 8,
                compiler_params=pltpu.CompilerParams(collective_id=0, has_side_effects=True), name="near_grads",
            )(cu_seqlens, q_loc, k_loc, v_loc, o_loc, do_loc, lse_loc.T)

        chip_pos = jnp.arange(1, n_dev // 2 - 1, dtype=jnp.int32)[:, None] * 2 * n_tok
        far = jnp.any((cu_seqlens[None, :-1] < chip_pos) & (cu_seqlens[None, 1:] > chip_pos + 2 * n_tok))
        return lax.cond(far, wide, near, q_loc, k_loc, v_loc, o_loc, do_loc, lse_loc, cu_seqlens)

    return jax.shard_map(device_fn, mesh=mesh, in_specs=(head_spec, head_spec, head_spec, head_spec, head_spec, row_spec, P()), out_specs=(head_spec, head_spec, head_spec), check_vma=False)
```

profile of v0, /device:TPU:3, one launch (start us, length us, event | category | flops | bytes accessed | tf_op | source)
XLA Modules:
  0.0 453.1 jit_solution(7163968884361105984)
XLA Ops:
  0.6 0.8 fusion.1
  1.4 0.7 and_reduce_fusion
  2.8 444.3 %conditional.1 = ((bf16[256,16,256]{2,1,0:T(8,128)(2,1)S(1)}, bf16[256,16,256]{2,1,0:T(8,128)(2,1)}, bf16[256,16,256]{2,1,0:T(8,128)(2,1)})) conditional(s32[]{:T(128)} %convert_element_type.12, (f32[256,16]{0,1:T(8,128)}, s32[67]{0:T(128)}, bf16[256,16,256]{2,1,0:T(8,128)(2,1)}, bf16[256,16,256]{2,1,0:T(8,128)(2,1)}, ...), branch_computations={%region_1.0_spmd, %region_2.4_spmd} | conditional | flops 8603682 | bytes 109245096 | solution.py:377
  3.0 0.8 select_reduce_fusion
  3.8 0.5 slice.14
  4.3 0.6 compare_convert_fusion
  5.0 0.1 convert_reduce_fusion
  5.1 0.6 pad_add_fusion.flag_ref
  5.7 2.3 bitcast_convert_fusion
  8.1 0.0 copy-start.8
  8.1 0.0 copy-start.2
  8.1 0.0 copy-start.3
  8.1 3.5 multiply_reduce_fusion
  11.7 0.0 copy-done.8
  11.7 0.6 pad_maximum_fusion.stat_ref
  12.3 0.0 copy-done.3
  12.3 1.6 copy_bitcast_fusion
  13.9 0.0 copy-start.1
  13.9 2.3 maximum_bitcast_fusion.1.kv_ref
  16.2 1.5 copy_bitcast_fusion.2
  17.7 2.3 maximum_bitcast_fusion.qd_ref
  20.0 362.8 %wide_exchange.1 = (bf16[6,2,16,256,256]{4,3,2,1,0:T(8,128)(2,1)}, f32[3,32,256]{2,1,0:T(8,128)}) custom-call(bf16[2,16,256,256]{3,2,1,0:T(8,128)(2,1)} %maximum_bitcast_fusion.1.kv_ref, bf16[2,16,256,256]{3,2,1,0:T(8,128)(2,1)} %maximum_bitcast_fusion.qd_ref, f32[32,256]{1,0:T(8,128)} %pad_maximum_fusion.stat_ref), custom_call_target="tpu_custom_call" | custom-call | tf_op jit(solution)/shard_map/cond/branch_1_fun/wide_exchange/pallas_call | solution.py:338
  382.8 56.3 %grads.1 = (bf16[16,256,256]{2,1,0:T(8,128)(2,1)}, bf16[16,256,256]{2,1,0:T(8,128)(2,1)}, bf16[16,256,256]{2,1,0:T(8,128)(2,1)}) custom-call(s32[7]{0:T(128)} %pad_add_fusion.flag_ref, bf16[2,16,256,256]{3,2,1,0:T(8,128)(2,1)} %maximum_bitcast_fusion.qd_ref, bf16[2,16,256,256]{3,2,1,0:T(8,128)(2,1)} %maximum_bitcast_fusion.1.kv_ref, ...), custom_call_target="tpu_custom_call" | custom-call | tf_op jit(solution)/shard_map/cond/branch_1_fun/grads/pallas_call | solution.py:345
  439.1 2.9 copy.54
  442.1 0.0 copy-start.4
  442.1 2.5 copy.56
  444.6 2.5 copy.58
  447.1 1.3 copy.74
  448.4 1.0 copy-done.6
  449.5 1.3 copy.75
  450.8 1.0 copy-done.7
  451.8 1.3 copy.76
  (15 shorter events, 0.0 us)
Async XLA Ops:
  3.8 4.2 copy-start.9
  5.7 2.3 copy-start
  8.1 3.6 copy-start.8
  8.1 4.2 copy-start.2
  8.1 4.2 copy-start.3
  13.9 2.3 copy-start.1
  439.1 2.9 copy-start.5
  442.1 2.6 copy-start.4
  447.1 2.3 copy-start.6
  449.5 2.3 copy-start.7
where the time goes:
time: 454 us; the launch traced here: 453 us
  Pallas kernels  419 us (92%)
  local copies, waits for them, and re-layouts  18.4 us (4%)
  other arithmetic  14 us (3%)
    pallas_call x1, Pallas kernels, wide(): pl.pallas_call(functools.partial(far_kernel, n_dev), out_shape=win_shapes...  363 us
    pallas_call x1, Pallas kernels, wide(): pl.pallas_call(functools.partial(grad_kernel, score_scale), grid_spec=plt...  56.3 us

commit v1 on v0

--- a/solution.py
+++ b/solution.py
@@ -10,6 +10,7 @@
 REACH = 3
 TILE_HEADS = 8
 ROW_PARTS = 2
+HEADS_AHEAD = 1
 LOG2E = 1.4426950408889634
 MESH_ID = pl.DeviceIdType.MESH
 
@@ -22,7 +23,10 @@
     barrier = pltpu.get_barrier_semaphore()
     for step in range(1, n_dev):
         pl.semaphore_signal(barrier, inc=1, device_id=to_dev(lax.rem(me + step, n_dev)), device_id_type=MESH_ID)
-    pl.semaphore_wait(barrier, n_dev - 1)
+
+
+def await_all(n_dev):
+    pl.semaphore_wait(pltpu.get_barrier_semaphore(), n_dev - 1)
 
 
 def stat_copies(me, n_dev, stat_ref, swin_ref, send_sem, recv_sem):
@@ -36,6 +40,7 @@
 def far_kernel(n_dev, kv_ref, qd_ref, stat_ref, win_ref, swin_ref, st_s, st_r, kv_s, kv_r, qd_s, qd_r):
     me = lax.axis_index("cp")
     greet_all(n_dev, me)
+    await_all(n_dev)
     stats = stat_copies(me, n_dev, stat_ref, swin_ref, st_s, st_r)
     for dist, copy in stats:
         up = pltpu.make_async_remote_copy(src_ref=kv_ref, dst_ref=win_ref.at[dist - 1], send_sem=kv_s.at[dist - 1], recv_sem=kv_r.at[dist - 1], device_id=to_dev(lax.rem(me + dist, n_dev)), device_id_type=MESH_ID)
@@ -156,14 +161,18 @@
     def own_qd(h):
         return remote(qd.at[:, h], win.at[4, :, h], own_s.at[h], own_r.at[h], mate)
 
-    def load(half, which):
+    halves = n_heads // TILE_HEADS
+    units = [(half, r) for half in range(halves) for r in range(ROW_PARTS)]
+
+    def load(half, r, which):
         src = (q_ref, k_ref, do_ref, v_ref)[which]
-        return pltpu.make_async_copy(src.at[:, pl.ds(half * TILE_HEADS, TILE_HEADS)], raw.at[half, which], ld_sem.at[half, which])
-
-    halves = n_heads // TILE_HEADS
-    for half in range(halves):
+        rows, heads = pl.ds(r * part, part), pl.ds(half * TILE_HEADS, TILE_HEADS)
+        return pltpu.make_async_copy(src.at[rows, heads], raw.at[half, which, rows], ld_sem.at[half, r, which])
+
+    greet_all(n_dev, me)
+    for half, r in units:
         for which in range(4):
-            load(half, which).start()
+            load(half, r, which).start()
     load_o = pltpu.make_async_copy(o_ref, raw_o, o_sem)
     load_o.start()
 
@@ -179,44 +188,48 @@
     found, cross_end = lax.fori_loop(0, cu_ref.shape[0] - 1, scan_docs, (jnp.zeros(starts.shape, jnp.int32), 0))
     starts[...] = jnp.where(pos < n_dev * n_tok, found, n_dev * n_tok)
     send_rows = jnp.clip(cross_end - base, 0, n_tok)
-    send_qd = lax.broadcasted_iota(jnp.int32, (TILE_HEADS, n_tok, q_ref.shape[2]), 1) < send_rows
-
-    greet_all(n_dev, me)
+    row_ids = lax.broadcasted_iota(jnp.int32, (TILE_HEADS, part, q_ref.shape[2]), 1)
     stats = stat_copies(me, n_dev, stat, swin, st_s, st_r)
 
-    def send_heads(half):
-        for h in range(half * TILE_HEADS, (half + 1) * TILE_HEADS):
-            for r in range(ROW_PARTS):
-                x_copy(h, r).start()
+    def arrange(half, r):
+        rows, heads = pl.ds(r * part, part), pl.ds(half * TILE_HEADS, TILE_HEADS)
+        for pair in range(2):
+            load(half, r, 2 * pair).wait()
+            load(half, r, 2 * pair + 1).wait()
+            q_side = jnp.swapaxes(raw[half, 2 * pair, rows], 0, 1)
+            k_side = jnp.swapaxes(raw[half, 2 * pair + 1, rows], 0, 1)
+            pk[pair, heads, rows] = jnp.where(row_ids < send_rows - r * part, q_side, k_side)
+            qd[pair, heads, rows] = q_side
+            kv[pair, heads, rows] = k_side
+
+    def start_own(half):
         for h in range(half * TILE_HEADS, (half + 1) * TILE_HEADS):
             pl.when(core == 0)(own_kv(h).start)
             pl.when(core == 1)(own_qd(h).start)
 
+    for r in range(ROW_PARTS):
+        arrange(0, r)
+        if r == 0:
+            await_all(n_dev)
+        x_copy(0, r).start()
+    start_own(0)
+    for half in range(1, halves):
+        for r in range(ROW_PARTS):
+            arrange(half, r)
+        start_own(half)
+    load_o.wait()
+    stat[0:n_heads, :] = lse_ref[...]
     for half in range(halves):
-        rows = pl.ds(half * TILE_HEADS, TILE_HEADS)
-        for pair in range(2):
-            load(half, 2 * pair).wait()
-            load(half, 2 * pair + 1).wait()
-            q_side = jnp.swapaxes(raw[half, 2 * pair], 0, 1)
-            k_side = jnp.swapaxes(raw[half, 2 * pair + 1], 0, 1)
-            pk[pair, rows] = jnp.where(send_qd, q_side, k_side)
-            qd[pair, rows] = q_side
-            kv[pair, rows] = k_side
-        if half == 0:
-            load_o.wait()
-            stat[0:n_heads, :] = lse_ref[...]
         delta = jnp.sum(raw[half, 2].astype(jnp.float32) * raw_o[:, half * TILE_HEADS:(half + 1) * TILE_HEADS, :].astype(jnp.float32), axis=-1)
         stat[n_heads + half * TILE_HEADS:n_heads + (half + 1) * TILE_HEADS, :] = delta.T
-        send_heads(half)
     for dist, copy in stats:
         pl.when(me >= dist)(copy.start)
-    for dist, copy in stats:
-        pl.when(me + dist < n_dev)(copy.wait_recv)
 
     terms = functools.partial(block_terms, score_scale)
 
     def arrive(h):
         for r in range(ROW_PARTS):
+            pl.when(h + HEADS_AHEAD < n_heads)(lambda: x_copy(h + HEADS_AHEAD, r).start())
             x_copy(h, r).wait_recv()
             pl.when(relays)(lambda: y_copy(h, r).start())
             fx_copy(h, r).start()
@@ -273,6 +286,12 @@
 
     def step(t, carry):
         pl.when(t < n_heads)(lambda: arrive(t))
+
+        @pl.when(t == 2)
+        def _():
+            for dist, copy in stats:
+                pl.when(me + dist < n_dev)(copy.wait_recv)
+
         pl.when(t >= 2)(lambda: compute(t - 2))
         for half in range(halves):
             @pl.when(t - 2 == (half + 1) * TILE_HEADS - 1)
@@ -367,7 +386,7 @@
                 + [pltpu.VMEM(pair_shape, bf16)] * 3 + [pltpu.VMEM((5,) + pair_shape, bf16)]
                 + [pltpu.VMEM((2 * n_heads, n_tok), f32), pltpu.VMEM((REACH, 2 * n_heads, n_tok), f32), pltpu.VMEM((8, n_tok), jnp.int32)]
                 + [pltpu.VMEM((3, TILE_HEADS, n_tok, head_dim), bf16)] + [pltpu.VMEM((n_tok, head_dim), f32)] * 3
-                + [dma((n_heads // TILE_HEADS, 4)), dma, dma((n_heads // TILE_HEADS, 3)), dma((REACH,)), dma((REACH,)), dma((n_heads,)), dma((n_heads,))]
+                + [dma((n_heads // TILE_HEADS, ROW_PARTS, 4)), dma, dma((n_heads // TILE_HEADS, 3)), dma((REACH,)), dma((REACH,)), dma((n_heads,)), dma((n_heads,))]
                 + [dma((n_heads, ROW_PARTS))] * 8,
                 compiler_params=pltpu.CompilerParams(collective_id=0, has_side_effects=True), name="near_grads",
             )(cu_seqlens, q_loc, k_loc, v_loc, o_loc, do_loc, lse_loc.T)

time: 454 us -> 122 us (0.27)
  Pallas kernels: 419 us -> 111 us
  other arithmetic: 14 us -> 0.71 us
  local copies, waits for them, and re-layouts: 18.4 us -> 6.81 us
    pallas_call x2 -> x1, Pallas kernels: 419 us -> 111 us  [near(): pl.pallas_call(functools.partial(near_kernel, n_dev, score_scale), out_sh...]
    cond x19 -> x0, local copies, waits for them, and re-layouts: 7.99 us -> none  [the longest x3 7.94 us: device_fn(): lax.cond(far, wide, near, q_loc, k_loc, v_loc, o_loc, do_loc, lse_loc, cu...]
    transpose x2 -> x0, other arithmetic: 4.6 us -> none  [the longest x1 2.32 us: wide(): qd = jnp.stack([q_loc, do_loc]).transpose(0, 2, 1, 3)]
where the time goes in v1:
time: 122 us; the launch traced here: 120 us
  Pallas kernels  111 us (91%)
  local copies, waits for them, and re-layouts  6.81 us (6%)
  between operations  1.31 us (1%)
    pallas_call x1, Pallas kernels, near(): pl.pallas_call(functools.partial(near_kernel, n_dev, score_scale), out_sh...  111 us
    unnamed x7, local copies, waits for them, and re-layouts  6.01 us

profile of v1, /device:TPU:3, one launch (start us, length us, event | category | flops | bytes accessed | tf_op | source)
XLA Modules:
  0.0 120.2 jit_solution(4906242358573344336)
XLA Ops:
  0.6 0.8 fusion.1
  1.4 0.7 and_reduce_fusion
  2.8 111.4 %conditional.1 = ((bf16[256,16,256]{2,1,0:T(8,128)(2,1)S(1)}, bf16[256,16,256]{2,1,0:T(8,128)(2,1)}, bf16[256,16,256]{2,1,0:T(8,128)(2,1)})) conditional(s32[]{:T(128)} %convert_element_type.12, (f32[256,16]{0,1:T(8,128)}, s32[67]{0:T(128)}, bf16[256,16,256]{2,1,0:T(8,128)(2,1)}, bf16[256,16,256]{2,1,0:T(8,128)(2,1)}, ...), branch_computations={%region_1.0_spmd, %region_2.4_spmd} | conditional | flops 8603682 | bytes 109245096 | solution.py:396
  2.8 111.1 %near_grads.1 = (bf16[256,16,256]{2,1,0:T(8,128)(2,1)S(1)}, bf16[256,16,256]{2,1,0:T(8,128)(2,1)}, bf16[256,16,256]{2,1,0:T(8,128)(2,1)}) custom-call(s32[67]{0:T(128)} %get-tuple-element.30.cu_ref, bf16[256,16,256]{2,1,0:T(8,128)(2,1)} %get-tuple-element.31.q_ref, bf16[256,16,256]{2,1,0:T(8,128)(2,1)} %get-tuple-element.32.k_ref, ...), custom_call_target="tpu_custom_call" | custom-call | tf_op jit(solution)/shard_map/cond/branch_0_fun/near_grads/pallas_call | solution.py:381
  114.2 0.0 copy-start.6
  114.2 1.3 %copy.74 = bf16[256,16,256]{2,1,0:T(8,128)(2,1)} copy(bf16[256,16,256]{2,1,0:T(8,128)(2,1)S(1)} %get-tuple-element.121) | data formatting | bytes 4194304
  115.5 1.0 copy-done.6
  116.5 0.0 copy-start.7
  116.5 1.3 %copy.75 = bf16[256,16,256]{2,1,0:T(8,128)(2,1)} copy(bf16[256,16,256]{2,1,0:T(8,128)(2,1)S(1)} %copy-done.6) | data formatting | bytes 4194304
  117.9 1.0 copy-done.7
  118.9 1.3 %copy.76 = bf16[256,16,256]{2,1,0:T(8,128)(2,1)} copy(bf16[256,16,256]{2,1,0:T(8,128)(2,1)S(1)} %copy-done.7) | data formatting | bytes 4194304
  (1 shorter events, 0.0 us)
Async XLA Ops:
  114.2 2.3 %copy-start.6 = (bf16[256,16,256]{2,1,0:T(8,128)(2,1)S(1)}, bf16[256,16,256]{2,1,0:T(8,128)(2,1)}, u32[]{:S(2)}) copy-start(bf16[256,16,256]{2,1,0:T(8,128)(2,1)} %get-tuple-element.122) | copy-start | bytes 6291460
  116.5 2.3 %copy-start.7 = (bf16[256,16,256]{2,1,0:T(8,128)(2,1)S(1)}, bf16[256,16,256]{2,1,0:T(8,128)(2,1)}, u32[]{:S(2)}) copy-start(bf16[256,16,256]{2,1,0:T(8,128)(2,1)} %get-tuple-element.123) | copy-start | bytes 6291460

commit v2 on v1

--- a/solution.py
+++ b/solution.py
@@ -35,28 +35,6 @@
         copy = pltpu.make_async_remote_copy(src_ref=stat_ref, dst_ref=swin_ref.at[dist - 1], send_sem=send_sem.at[dist - 1], recv_sem=recv_sem.at[dist - 1], device_id=to_dev(lax.rem(me + n_dev - dist, n_dev)), device_id_type=MESH_ID)
         out.append((dist, copy))
     return out
-
-
-def far_kernel(n_dev, kv_ref, qd_ref, stat_ref, win_ref, swin_ref, st_s, st_r, kv_s, kv_r, qd_s, qd_r):
-    me = lax.axis_index("cp")
-    greet_all(n_dev, me)
-    await_all(n_dev)
-    stats = stat_copies(me, n_dev, stat_ref, swin_ref, st_s, st_r)
-    for dist, copy in stats:
-        up = pltpu.make_async_remote_copy(src_ref=kv_ref, dst_ref=win_ref.at[dist - 1], send_sem=kv_s.at[dist - 1], recv_sem=kv_r.at[dist - 1], device_id=to_dev(lax.rem(me + dist, n_dev)), device_id_type=MESH_ID)
-        down = pltpu.make_async_remote_copy(src_ref=qd_ref, dst_ref=win_ref.at[REACH + dist - 1], send_sem=qd_s.at[dist - 1], recv_sem=qd_r.at[dist - 1], device_id=to_dev(lax.rem(me + n_dev - dist, n_dev)), device_id_type=MESH_ID)
-        pl.when(me + dist < n_dev)(up.start)
-        pl.when(me >= dist)(down.start)
-        pl.when(me >= dist)(copy.start)
-    for dist, copy in stats:
-        up = pltpu.make_async_remote_copy(src_ref=kv_ref, dst_ref=win_ref.at[dist - 1], send_sem=kv_s.at[dist - 1], recv_sem=kv_r.at[dist - 1], device_id=to_dev(lax.rem(me + dist, n_dev)), device_id_type=MESH_ID)
-        down = pltpu.make_async_remote_copy(src_ref=qd_ref, dst_ref=win_ref.at[REACH + dist - 1], send_sem=qd_s.at[dist - 1], recv_sem=qd_r.at[dist - 1], device_id=to_dev(lax.rem(me + n_dev - dist, n_dev)), device_id_type=MESH_ID)
-        pl.when(me + dist < n_dev)(up.wait_send)
-        pl.when(me >= dist)(up.wait_recv)
-        pl.when(me >= dist)(down.wait_send)
-        pl.when(me + dist < n_dev)(down.wait_recv)
-        pl.when(me >= dist)(copy.wait_send)
-        pl.when(me + dist < n_dev)(copy.wait_recv)
 
 
 def nt_dot(a, b):
@@ -82,40 +60,66 @@
     return p_t.astype(jnp.bfloat16), ds_t
 
 
-def grad_kernel(score_scale, flag_ref, qd_ref, kv_ref, win_ref, stat_ref, swin_ref, start_ref, dq_ref, dk_ref, dv_ref, dq_acc, dk_acc, dv_acc):
+def swap_kernel(n_dev, pairs, *refs):
+    me = lax.axis_index("cp")
+    views = pairs(refs[:-3])
+    s_sem, r_sem, l_sem = refs[-3:]
+    greet_all(n_dev, me)
+    await_all(n_dev)
+
+    def copies(mask):
+        peer = me ^ mask
+        return [pltpu.make_async_remote_copy(src_ref=src(peer), dst_ref=dst(me), send_sem=s_sem.at[n, mask], recv_sem=r_sem.at[n, mask], device_id=to_dev(peer), device_id_type=MESH_ID)
+                for n, (src, dst) in enumerate(views)]
+
+    order = [2, 4, 6, 3, 5, 7, 1]
+    for mask in order:
+        for copy in copies(mask):
+            copy.start()
+    for n, (src, dst) in enumerate(views):
+        pltpu.make_async_copy(src(me), dst(me), l_sem.at[n]).start()
+    for n, (src, dst) in enumerate(views):
+        pltpu.make_async_copy(src(me), dst(me), l_sem.at[n]).wait()
+    for mask in order:
+        for copy in copies(mask):
+            copy.wait()
+
+
+def head_kernel(score_scale, start_ref, got_ref, gstat_ref, rows_ref, out_ref, dq_acc, dk_acc, dv_acc):
     head = pl.program_id(0)
-    n_heads = pl.num_programs(0)
-    base = flag_ref[2 * REACH]
-    n_tok = qd_ref.shape[2]
-
+    n_dev, _, _, n_tok, _ = got_ref.shape
     terms = functools.partial(block_terms, score_scale)
 
-    q_blk, do_blk = qd_ref[0, 0], qd_ref[1, 0]
-    k_blk, v_blk = kv_ref[0, 0], kv_ref[1, 0]
-    lse_own, delta_own = stat_ref[pl.ds(head, 1), :], stat_ref[pl.ds(n_heads + head, 1), :]
-    p_t, ds_t = terms(k_blk, v_blk, q_blk, do_blk, lse_own, delta_own, start_ref[0:1, :], base, base)
-    dv_acc[...] = nn_dot(p_t, do_blk)
-    dk_acc[...] = nn_dot(ds_t, q_blk)
-    dq_acc[...] = tn_dot(ds_t, k_blk)
-    for dist in range(1, REACH + 1):
-        @pl.when(flag_ref[dist - 1] == 1)
-        def _():
-            k_far, v_far = win_ref[dist - 1, 0, 0], win_ref[dist - 1, 1, 0]
-            _, ds_far = terms(k_far, v_far, q_blk, do_blk, lse_own, delta_own, start_ref[0:1, :], base - dist * n_tok, base)
-            dq_acc[...] += tn_dot(ds_far, k_far)
-
-        @pl.when(flag_ref[REACH + dist - 1] == 1)
-        def _():
-            q_far, do_far = win_ref[REACH + dist - 1, 0, 0], win_ref[REACH + dist - 1, 1, 0]
-            lse_far = swin_ref[dist - 1, pl.ds(head, 1), :]
-            delta_far = swin_ref[dist - 1, pl.ds(n_heads + head, 1), :]
-            p_far, ds_far = terms(k_blk, v_blk, q_far, do_far, lse_far, delta_far, start_ref[dist:dist + 1, :], base, base + dist * n_tok)
-            dv_acc[...] += nn_dot(p_far, do_far)
-            dk_acc[...] += nn_dot(ds_far, q_far)
-
-    dq_ref[0] = (dq_acc[...] * score_scale).astype(dq_ref.dtype)
-    dk_ref[0] = (dk_acc[...] * score_scale).astype(dk_ref.dtype)
-    dv_ref[0] = dv_acc[...].astype(dv_ref.dtype)
+    def shard(i, carry):
+        q_blk, do_blk = got_ref[i, 0, 0], got_ref[i, 3, 0]
+        lse_row, delta_row = gstat_ref[i, pl.ds(head, 1), :], gstat_ref[i, pl.ds(2 + head, 1), :]
+        start_row = rows_ref[pl.ds(i, 1), :]
+
+        def pair(j, first):
+            k_blk, v_blk = got_ref[j, 1, 0], got_ref[j, 2, 0]
+            p_t, ds_t = terms(k_blk, v_blk, q_blk, do_blk, lse_row, delta_row, start_row, j * n_tok, i * n_tok)
+            dv, dk, dq = nn_dot(p_t, do_blk), nn_dot(ds_t, q_blk), tn_dot(ds_t, k_blk)
+            if first:
+                dv_acc[j], dk_acc[j], dq_acc[i] = dv, dk, dq
+            else:
+                dv_acc[j] += dv
+                dk_acc[j] += dk
+                dq_acc[i] += dq
+
+        pair(i, True)
+        lowest = start_ref[i] // n_tok
+        lax.fori_loop(lowest, i, lambda j, c: (pair(j, False), c)[1], 0)
+        return carry
+
+    lax.fori_loop(0, n_dev, shard, 0)
+
+    def write(i, carry):
+        out_ref[i, 0, 0] = (dq_acc[i] * score_scale).astype(out_ref.dtype)
+        out_ref[i, 1, 0] = (dk_acc[i] * score_scale).astype(out_ref.dtype)
+        out_ref[i, 2, 0] = dv_acc[i].astype(out_ref.dtype)
+        return carry
+
+    lax.fori_loop(0, n_dev, write, 0)
 
 
 def near_kernel(n_dev, score_scale, cu_ref, q_ref, k_ref, v_ref, o_ref, do_ref, lse_ref, dq_ref, dk_ref, dv_ref,
@@ -335,45 +339,47 @@
         n_tok, n_heads, head_dim = q_loc.shape
         seq_len = n_tok * n_dev
         score_scale = head_dim ** -0.5
-        me = lax.axis_index("cp")
         pair_shape = (2, n_heads, n_tok, head_dim)
 
         def wide(q_loc, k_loc, v_loc, o_loc, do_loc, lse_loc, cu_seqlens):
-            def doc_start(pos):
-                found = jnp.max(jnp.where(cu_seqlens <= pos[..., None], cu_seqlens, 0), axis=-1)
-                return jnp.where(pos < seq_len, found, seq_len).astype(jnp.int32)
-
-            base = me * n_tok
-            start_rows = doc_start(base + jnp.arange((REACH + 1) * n_tok, dtype=jnp.int32)).reshape(REACH + 1, n_tok)
-            dists = jnp.arange(1, REACH + 1, dtype=jnp.int32)
-            kv_on = start_rows[0, 0] < base - (dists - 1) * n_tok
-            qd_on = start_rows[1:, 0] < base + n_tok
-            flags = jnp.concatenate([kv_on.astype(jnp.int32), qd_on.astype(jnp.int32), base[None]]).astype(jnp.int32)
-            delta_loc = jnp.einsum("shd,shd->sh", do_loc, o_loc, preferred_element_type=jnp.float32)
-            stat = jnp.concatenate([lse_loc.T, delta_loc.T])
-            qd = jnp.stack([q_loc, do_loc]).transpose(0, 2, 1, 3)
-            kv = jnp.stack([k_loc, v_loc]).transpose(0, 2, 1, 3)
-            win_shapes = (jax.ShapeDtypeStruct((2 * REACH,) + qd.shape, qd.dtype), jax.ShapeDtypeStruct((REACH,) + stat.shape, stat.dtype))
-            win, swin = pl.pallas_call(functools.partial(far_kernel, n_dev), out_shape=win_shapes, in_specs=[any_spec] * 3, out_specs=(any_spec, any_spec),
-                                       scratch_shapes=[dma((REACH,))] * 6,
-                                       compiler_params=pltpu.CompilerParams(collective_id=1, has_side_effects=True), name="wide_exchange")(kv, qd, stat)
-            head_blk = lambda h, flag: (0, h, 0, 0)
-            full2 = lambda h, flag: (0, 0)
-            out_blk = pl.BlockSpec((1, n_tok, head_dim), lambda h, flag: (h, 0, 0))
-            out_one = jax.ShapeDtypeStruct((n_heads, n_tok, head_dim), jnp.bfloat16)
-            dq, dk, dv = pl.pallas_call(
-                functools.partial(grad_kernel, score_scale),
+            bf16, f32 = jnp.bfloat16, jnp.float32
+            per = n_heads // n_dev
+            pos = jnp.arange(seq_len, dtype=jnp.int32).reshape(n_dev, n_tok)
+            start_rows = jnp.max(jnp.where(cu_seqlens <= pos[..., None], cu_seqlens, 0), axis=-1)
+            delta_loc = jnp.einsum("shd,shd->hs", do_loc, o_loc, preferred_element_type=f32)
+            parts = [item.reshape(n_dev, per, n_tok) for item in (lse_loc.T, delta_loc)]
+            stat = jnp.concatenate(parts + [jnp.zeros((n_dev, 8 - 2 * per, n_tok), f32)], axis=1)
+            ops = jnp.stack([q_loc, k_loc, v_loc, do_loc]).transpose(0, 2, 1, 3)
+
+            def heads_of(dev):
+                return pl.ds(dev * per, per)
+
+            def call(pairs, n_pairs, ident, out_shape, *args):
+                return pl.pallas_call(functools.partial(swap_kernel, n_dev, pairs), out_shape=out_shape,
+                                      in_specs=[any_spec] * len(args), out_specs=[any_spec] * len(out_shape),
+                                      scratch_shapes=[dma((n_pairs, n_dev)), dma((n_pairs, n_dev)), dma((n_pairs,))],
+                                      compiler_params=pltpu.CompilerParams(collective_id=ident, has_side_effects=True))(*args)
+
+            def in_pairs(refs):
+                ops_ref, stat_ref, got_ref, gstat_ref = refs
+                return [(lambda d: ops_ref.at[:, heads_of(d)], lambda d: got_ref.at[d]), (lambda d: stat_ref.at[d], lambda d: gstat_ref.at[d])]
+
+            def out_pairs(refs):
+                grad_ref, back_ref = refs
+                return [(lambda d: grad_ref.at[d], lambda d: back_ref.at[:, heads_of(d)])]
+
+            got, gstat = call(in_pairs, 2, 1, (jax.ShapeDtypeStruct((n_dev, 4, per, n_tok, head_dim), bf16), jax.ShapeDtypeStruct((n_dev, 8, n_tok), f32)), ops, stat)
+            grads = pl.pallas_call(
+                functools.partial(head_kernel, score_scale),
                 grid_spec=pltpu.PrefetchScalarGridSpec(
-                    num_scalar_prefetch=1, grid=(n_heads,),
-                    in_specs=[pl.BlockSpec((2, 1, n_tok, head_dim), head_blk), pl.BlockSpec((2, 1, n_tok, head_dim), head_blk),
-                              pl.BlockSpec((2 * REACH, 2, 1, n_tok, head_dim), lambda h, flag: (0, 0, h, 0, 0)),
-                              pl.BlockSpec(stat.shape, full2), pl.BlockSpec((REACH,) + stat.shape, lambda h, flag: (0, 0, 0)),
-                              pl.BlockSpec((REACH + 1, n_tok), full2)],
-                    out_specs=[out_blk] * 3,
-                    scratch_shapes=[pltpu.VMEM((n_tok, head_dim), jnp.float32)] * 3),
-                out_shape=(out_one, out_one, out_one), name="grads",
-            )(flags, qd, kv, win, stat, swin, start_rows)
-            return tuple(item.transpose(1, 0, 2) for item in (dq, dk, dv))
+                    num_scalar_prefetch=1, grid=(per,),
+                    in_specs=[pl.BlockSpec((n_dev, 4, 1, n_tok, head_dim), lambda h, s: (0, 0, h, 0, 0)), pl.BlockSpec((n_dev, 8, n_tok), lambda h, s: (0, 0, 0)), pl.BlockSpec((n_dev, n_tok), lambda h, s: (0, 0))],
+                    out_specs=pl.BlockSpec((n_dev, 3, 1, n_tok, head_dim), lambda h, s: (0, 0, h, 0, 0)),
+                    scratch_shapes=[pltpu.VMEM((n_dev, n_tok, head_dim), f32)] * 3),
+                out_shape=jax.ShapeDtypeStruct((n_dev, 3, per, n_tok, head_dim), bf16), name="head_grads",
+            )(start_rows[:, 0], got, gstat, start_rows)
+            back, = call(out_pairs, 1, 2, (jax.ShapeDtypeStruct((3, n_heads, n_tok, head_dim), bf16),), grads)
+            return tuple(back[n].transpose(1, 0, 2) for n in range(3))
 
         def near(q_loc, k_loc, v_loc, o_loc, do_loc, lse_loc, cu_seqlens):
             out_one = jax.ShapeDtypeStruct(q_loc.shape, q_loc.dtype)
@@ -392,7 +398,8 @@
             )(cu_seqlens, q_loc, k_loc, v_loc, o_loc, do_loc, lse_loc.T)
 
         chip_pos = jnp.arange(1, n_dev // 2 - 1, dtype=jnp.int32)[:, None] * 2 * n_tok
-        far = jnp.any((cu_seqlens[None, :-1] < chip_pos) & (cu_seqlens[None, 1:] > chip_pos + 2 * n_tok))
+        cuts = (cu_seqlens[None] >= chip_pos) & (cu_seqlens[None] <= chip_pos + 2 * n_tok)
+        far = jnp.logical_not(jnp.all(jnp.any(cuts, axis=1)))
         return lax.cond(far, wide, near, q_loc, k_loc, v_loc, o_loc, do_loc, lse_loc, cu_seqlens)
 
     return jax.shard_map(device_fn, mesh=mesh, in_specs=(head_spec, head_spec, head_spec, head_spec, head_spec, row_spec, P()), out_specs=(head_spec, head_spec, head_spec), check_vma=False)

time: 122 us -> 121 us (level)
  no operation moved by 1% of the time
where the time goes in v2:
time: 121 us; the launch traced here: 120 us
  Pallas kernels  111 us (92%)
  local copies, waits for them, and re-layouts  6.01 us (5%)
  other arithmetic  1.49 us (1%)
  between operations  1.31 us (1%)
    pallas_call x1, Pallas kernels, near(): pl.pallas_call(functools.partial(near_kernel, n_dev, score_scale), out_sh...  111 us
    unnamed x7, local copies, waits for them, and re-layouts  6.01 us

profile of v2, /device:TPU:3, one launch (start us, length us, event | category | flops | bytes accessed | tf_op | source)
XLA Modules:
  0.0 120.2 jit_solution(469792786898359278)
XLA Ops:
  0.6 0.8 and_reduce_fusion
  1.5 0.6 reduce_and.9
  2.8 111.4 %conditional.1 = ((bf16[256,16,256]{2,1,0:T(8,128)(2,1)S(1)}, bf16[256,16,256]{2,1,0:T(8,128)(2,1)}, bf16[256,16,256]{2,1,0:T(8,128)(2,1)})) conditional(s32[]{:T(128)} %convert_element_type.3, (f32[256,16]{0,1:T(8,128)}, s32[67]{0:T(128)}, bf16[256,16,256]{2,1,0:T(8,128)(2,1)}, bf16[256,16,256]{2,1,0:T(8,128)(2,1)}, bf16[256,16,256]{2,1,0:T(8,128)(2,1)}, ...), branch_computations={%region_2.0_spmd, %region_3.5_spmd} | conditional | flops 17219584 | bytes 105195208 | solution.py:403
  2.8 111.1 %near_grads.1 = (bf16[256,16,256]{2,1,0:T(8,128)(2,1)S(1)}, bf16[256,16,256]{2,1,0:T(8,128)(2,1)}, bf16[256,16,256]{2,1,0:T(8,128)(2,1)}) custom-call(s32[67]{0:T(128)} %get-tuple-element.28.cu_ref, bf16[256,16,256]{2,1,0:T(8,128)(2,1)} %get-tuple-element.29.q_ref, bf16[256,16,256]{2,1,0:T(8,128)(2,1)} %get-tuple-element.30.k_ref, ...), custom_call_target="tpu_custom_call" | custom-call | tf_op jit(solution)/shard_map/cond/branch_0_fun/near_grads/pallas_call | solution.py:387
  114.1 0.0 copy-start.4
  114.1 1.3 %copy.75 = bf16[256,16,256]{2,1,0:T(8,128)(2,1)} copy(bf16[256,16,256]{2,1,0:T(8,128)(2,1)S(1)} %get-tuple-element.113) | data formatting | bytes 4194304
  115.5 1.0 copy-done.4
  116.5 0.0 copy-start.5
  116.5 1.3 %copy.76 = bf16[256,16,256]{2,1,0:T(8,128)(2,1)} copy(bf16[256,16,256]{2,1,0:T(8,128)(2,1)S(1)} %copy-done.4) | data formatting | bytes 4194304
  117.8 1.0 copy-done.5
  118.8 1.3 %copy.77 = bf16[256,16,256]{2,1,0:T(8,128)(2,1)} copy(bf16[256,16,256]{2,1,0:T(8,128)(2,1)S(1)} %copy-done.5) | data formatting | bytes 4194304
  (1 shorter events, 0.0 us)
Async XLA Ops:
  114.1 2.3 %copy-start.4 = (bf16[256,16,256]{2,1,0:T(8,128)(2,1)S(1)}, bf16[256,16,256]{2,1,0:T(8,128)(2,1)}, u32[]{:S(2)}) copy-start(bf16[256,16,256]{2,1,0:T(8,128)(2,1)} %get-tuple-element.114) | copy-start | bytes 6291460
  116.5 2.3 %copy-start.5 = (bf16[256,16,256]{2,1,0:T(8,128)(2,1)S(1)}, bf16[256,16,256]{2,1,0:T(8,128)(2,1)}, u32[]{:S(2)}) copy-start(bf16[256,16,256]{2,1,0:T(8,128)(2,1)} %get-tuple-element.115) | copy-start | bytes 6291460

commit v3 on v2

--- a/solution.py
+++ b/solution.py
@@ -10,7 +10,8 @@
 REACH = 3
 TILE_HEADS = 8
 ROW_PARTS = 2
-HEADS_AHEAD = 1
+IN_FLIGHT = 4
+OUT_STEPS = 2
 LOG2E = 1.4426950408889634
 MESH_ID = pl.DeviceIdType.MESH
 
@@ -123,7 +124,7 @@
 
 
 def near_kernel(n_dev, score_scale, cu_ref, q_ref, k_ref, v_ref, o_ref, do_ref, lse_ref, dq_ref, dk_ref, dv_ref,
-                raw, raw_o, qd, kv, pk, win, stat, swin, starts, out_hm, dq_acc, dk_acc, dv_acc,
+                raw, raw_o, qd, kv, pk, win, stat, swin, starts, out_buf, dq_acc, dk_acc, dv_acc,
                 ld_sem, o_sem, out_sem, st_s, st_r, own_s, own_r, x_s, x_r, y_s, y_r, fx_s, fx_r, fy_s, fy_r):
     me = lax.axis_index("cp")
     core = lax.rem(me, 2)
@@ -153,11 +154,11 @@
     def y_copy(h, r):
         return remote(block(x_slot, h, r), block(y_slot, h, r), y_s.at[h, r], y_r.at[h, r], y_dev)
 
-    def fx_copy(h, r):
-        return remote(block(x_slot, h, r), block(4 - 2 * core - 2 * chip_odd, h, r), fx_s.at[h, r], fx_r.at[h, r], mate)
-
-    def fy_copy(h, r):
-        return remote(block(y_slot, h, r), block(2 - 2 * core + 2 * chip_odd, h, r), fy_s.at[h, r], fy_r.at[h, r], mate)
+    def fx_copy(h):
+        return remote(win.at[x_slot, :, h], win.at[4 - 2 * core - 2 * chip_odd, :, h], fx_s.at[h], fx_r.at[h], mate)
+
+    def fy_copy(h):
+        return remote(win.at[y_slot, :, h], win.at[2 - 2 * core + 2 * chip_odd, :, h], fy_s.at[h], fy_r.at[h], mate)
 
     def own_kv(h):
         return remote(kv.at[:, h], win.at[0, :, h], own_s.at[h], own_r.at[h], mate)
@@ -181,17 +182,22 @@
     load_o.start()
 
     chip_pos = chip * 2 * n_tok
-    pos = base + n_tok * lax.broadcasted_iota(jnp.int32, starts.shape, 0) + lax.broadcasted_iota(jnp.int32, starts.shape, 1)
-
-    def scan_docs(n, carry):
-        found, cross_end = carry
-        first, last = cu_ref[n], cu_ref[n + 1]
-        crosses = (first < chip_pos) & (last > chip_pos)
-        return jnp.where(first <= pos, jnp.maximum(found, first), found), jnp.where(crosses, last, cross_end)
-
-    found, cross_end = lax.fori_loop(0, cu_ref.shape[0] - 1, scan_docs, (jnp.zeros(starts.shape, jnp.int32), 0))
-    starts[...] = jnp.where(pos < n_dev * n_tok, found, n_dev * n_tok)
-    send_rows = jnp.clip(cross_end - base, 0, n_tok)
+
+    def scan_cross(n, cross_end):
+        return jnp.where((cu_ref[n] < chip_pos) & (cu_ref[n + 1] > chip_pos), cu_ref[n + 1], cross_end)
+
+    n_docs = cu_ref.shape[0] - 1
+    send_rows = lax.fori_loop(0, n_docs, scan_cross, 0, unroll=True) - base
+
+    def find_starts():
+        pos = base + n_tok * lax.broadcasted_iota(jnp.int32, starts.shape, 0) + lax.broadcasted_iota(jnp.int32, starts.shape, 1)
+
+        def scan_docs(n, found):
+            return jnp.where(cu_ref[n] <= pos, jnp.maximum(found, cu_ref[n]), found)
+
+        found = lax.fori_loop(0, n_docs, scan_docs, jnp.zeros(starts.shape, jnp.int32))
+        starts[...] = jnp.where(pos < n_dev * n_tok, found, n_dev * n_tok)
+
     row_ids = lax.broadcasted_iota(jnp.int32, (TILE_HEADS, part, q_ref.shape[2]), 1)
     stats = stat_copies(me, n_dev, stat, swin, st_s, st_r)
 
@@ -221,6 +227,7 @@
         for r in range(ROW_PARTS):
             arrange(half, r)
         start_own(half)
+    find_starts()
     load_o.wait()
     stat[0:n_heads, :] = lse_ref[...]
     for half in range(halves):
@@ -233,97 +240,115 @@
 
     def arrive(h):
         for r in range(ROW_PARTS):
-            pl.when(h + HEADS_AHEAD < n_heads)(lambda: x_copy(h + HEADS_AHEAD, r).start())
             x_copy(h, r).wait_recv()
             pl.when(relays)(lambda: y_copy(h, r).start())
-            fx_copy(h, r).start()
+            pl.when(h + 1 < n_heads)(lambda: x_copy(h + 1, r).start())
+        fx_copy(h).start()
 
     def arrive_y(h):
         for r in range(ROW_PARTS):
             y_copy(h, r).wait_recv()
-            fy_copy(h, r).start()
-
-    def compute(h):
+        fy_copy(h).start()
+
+    def mine(h):
+        return qd[0, h], qd[1, h], kv[0, h], kv[1, h]
+
+    def key_block(h, slot):
+        q_blk, do_blk, _, _ = mine(h)
+        k_far, v_far = win[slot, 0, h], win[slot, 1, h]
+        _, ds_far = terms(k_far, v_far, q_blk, do_blk, stat[pl.ds(h, 1), :], stat[pl.ds(n_heads + h, 1), :], starts[0:1, :], base - (slot + 1) * n_tok, base)
+        return tn_dot(ds_far, k_far)
+
+    def query_block(h, slot):
+        _, _, k_blk, v_blk = mine(h)
+        dist = 5 - slot
+        q_far, do_far = win[slot, 0, h], win[slot, 1, h]
+        p_far, ds_far = terms(k_blk, v_blk, q_far, do_far, swin[dist - 1, pl.ds(h, 1), :], swin[dist - 1, pl.ds(n_heads + h, 1), :], starts[pl.ds(dist, 1), :], base, base + dist * n_tok)
+        return nn_dot(ds_far, q_far), nn_dot(p_far, do_far)
+
+    def key_blocks(h, slots):
+        dq_acc[h % IN_FLIGHT] += sum(key_block(h, slot) for slot in slots)
+
+    def query_blocks(h, slots):
+        found = [query_block(h, slot) for slot in slots]
+        dk_acc[h % IN_FLIGHT] += sum(item[0] for item in found)
+        dv_acc[h % IN_FLIGHT] += sum(item[1] for item in found)
+
+    def chip_part(h):
+        q_blk, do_blk, k_blk, v_blk = mine(h)
+        p_t, ds_t = terms(k_blk, v_blk, q_blk, do_blk, stat[pl.ds(h, 1), :], stat[pl.ds(n_heads + h, 1), :], starts[0:1, :], base, base)
+        dv_acc[h % IN_FLIGHT] = nn_dot(p_t, do_blk)
+        dk_acc[h % IN_FLIGHT] = nn_dot(ds_t, q_blk)
+        dq_acc[h % IN_FLIGHT] = tn_dot(ds_t, k_blk)
         own_qd(h).wait_recv()
-        for r in range(ROW_PARTS):
-            fx_copy(h, r).wait_recv()
-
-        @pl.when(middle)
+        pl.when(core == 1)(lambda: key_blocks(h, [0]))
+        pl.when(core == 0)(lambda: query_blocks(h, [4]))
+
+    def far_part(h, keys):
+        pl.when(keys)(lambda: key_blocks(h, [1, 2 * core]))
+        pl.when(jnp.logical_not(keys))(lambda: query_blocks(h, [3, 2 + 2 * core]))
+
+    def x_part(h):
+        fx_copy(h).wait_recv()
+        far_part(h, chip_odd == 1)
+
+    def y_part(h):
+        fy_copy(h).wait_recv()
+        far_part(h, chip_odd == 0)
+
+    def out_copy(h, which):
+        dst = (dq_ref, dk_ref, dv_ref)[which]
+        return pltpu.make_async_copy(out_buf.at[h % IN_FLIGHT, which], dst.at[h], out_sem.at[h % IN_FLIGHT, which])
+
+    def finish(h):
+        @pl.when(h >= IN_FLIGHT)
         def _():
-            for r in range(ROW_PARTS):
-                fy_copy(h, r).wait_recv()
-
-        q_blk, do_blk, k_blk, v_blk = qd[0, h], qd[1, h], kv[0, h], kv[1, h]
-        lse_own, delta_own = stat[pl.ds(h, 1), :], stat[pl.ds(n_heads + h, 1), :]
-        p_t, ds_t = terms(k_blk, v_blk, q_blk, do_blk, lse_own, delta_own, starts[0:1, :], base, base)
-        dv_acc[...] = nn_dot(p_t, do_blk)
-        dk_acc[...] = nn_dot(ds_t, q_blk)
-        dq_acc[...] = tn_dot(ds_t, k_blk)
-        for dist in range(1, REACH + 1):
-            k_here = {1: (core == 1) | not_first, 2: not_first, 3: (core == 1) & not_first}[dist]
-            q_here = {1: (core == 0) | not_last, 2: not_last, 3: (core == 0) & not_last}[dist]
-
-            @pl.when(k_here)
-            def _():
-                k_far, v_far = win[dist - 1, 0, h], win[dist - 1, 1, h]
-                _, ds_far = terms(k_far, v_far, q_blk, do_blk, lse_own, delta_own, starts[0:1, :], base - dist * n_tok, base)
-                dq_acc[...] += tn_dot(ds_far, k_far)
-
-            @pl.when(q_here)
-            def _():
-                q_far, do_far = win[5 - dist, 0, h], win[5 - dist, 1, h]
-                lse_far = swin[dist - 1, pl.ds(h, 1), :]
-                delta_far = swin[dist - 1, pl.ds(n_heads + h, 1), :]
-                p_far, ds_far = terms(k_blk, v_blk, q_far, do_far, lse_far, delta_far, starts[dist:dist + 1, :], base, base + dist * n_tok)
-                dv_acc[...] += nn_dot(p_far, do_far)
-                dk_acc[...] += nn_dot(ds_far, q_far)
-
-        h_in = lax.rem(h, TILE_HEADS)
-        out_hm[0, h_in] = (dq_acc[...] * score_scale).astype(out_hm.dtype)
-        out_hm[1, h_in] = (dk_acc[...] * score_scale).astype(out_hm.dtype)
-        out_hm[2, h_in] = dv_acc[...].astype(out_hm.dtype)
-
-    def out_copy(half, which):
-        dst = (dq_ref, dk_ref, dv_ref)[which]
-        rows = pl.ds(half * TILE_HEADS, TILE_HEADS)
-        return pltpu.make_async_copy(raw.at[half, which], dst.at[:, rows], out_sem.at[half, which])
+            for which in range(3):
+                out_copy(h - IN_FLIGHT, which).wait()
+
+        at = h % IN_FLIGHT
+        out_buf[at, 0] = (dq_acc[at] * score_scale).astype(out_buf.dtype)
+        out_buf[at, 1] = (dk_acc[at] * score_scale).astype(out_buf.dtype)
+        out_buf[at, 2] = dv_acc[at].astype(out_buf.dtype)
+        for which in range(3):
+            out_copy(h, which).start()
+
+    for dist, copy in stats:
+        pl.when(me + dist < n_dev)(copy.wait_recv)
+    chip_part(0)
 
     def step(t, carry):
         pl.when(t < n_heads)(lambda: arrive(t))
 
-        @pl.when(t == 2)
-        def _():
-            for dist, copy in stats:
-                pl.when(me + dist < n_dev)(copy.wait_recv)
-
-        pl.when(t >= 2)(lambda: compute(t - 2))
-        for half in range(halves):
-            @pl.when(t - 2 == (half + 1) * TILE_HEADS - 1)
-            def _():
-                for which in range(3):
-                    raw[half, which] = jnp.swapaxes(out_hm[which], 0, 1)
-                for which in range(3):
-                    out_copy(half, which).start()
+        pl.when((t >= 1) & (t <= n_heads))(lambda: x_part(t - 1))
         pl.when((t >= 1) & (t <= n_heads) & middle)(lambda: arrive_y(t - 1))
+        pl.when((t >= 2) & middle)(lambda: y_part(t - 2))
+        pl.when(t >= 2)(lambda: finish(t - 2))
+        pl.when(t < n_heads - 1)(lambda: chip_part(t + 1))
         return carry
 
     lax.fori_loop(0, n_heads + 2, step, 0)
 
     def drain(h, carry):
         own_kv(h).wait_send()
+        fx_copy(h).wait_send()
+        pl.when(middle)(lambda: fy_copy(h).wait_send())
         for r in range(ROW_PARTS):
             x_copy(h, r).wait_send()
-            fx_copy(h, r).wait_send()
             pl.when(relays)(lambda: y_copy(h, r).wait_send())
-            pl.when(middle)(lambda: fy_copy(h, r).wait_send())
         return carry
 
     lax.fori_loop(0, n_heads, drain, 0)
     for dist, copy in stats:
         pl.when(me >= dist)(copy.wait_send)
-    for half in range(halves):
+    for h in range(n_heads - IN_FLIGHT, n_heads):
         for which in range(3):
-            out_copy(half, which).wait()
+            out_copy(h, which).wait()
+
+
+def token_major_kernel(dq_ref, dk_ref, dv_ref, dq_out, dk_out, dv_out):
+    for src, dst in ((dq_ref, dq_out), (dk_ref, dk_out), (dv_ref, dv_out)):
+        dst[...] = jnp.swapaxes(src[...], 0, 1)
 
 
 def solution(mesh):
@@ -382,24 +407,37 @@
             return tuple(back[n].transpose(1, 0, 2) for n in range(3))
 
         def near(q_loc, k_loc, v_loc, o_loc, do_loc, lse_loc, cu_seqlens):
-            out_one = jax.ShapeDtypeStruct(q_loc.shape, q_loc.dtype)
+            out_one = jax.ShapeDtypeStruct((n_heads, n_tok, head_dim), q_loc.dtype)
             bf16, f32 = jnp.bfloat16, jnp.float32
-            return pl.pallas_call(
+            heads_out = pl.pallas_call(
                 functools.partial(near_kernel, n_dev, score_scale),
                 out_shape=(out_one, out_one, out_one),
                 in_specs=[smem_spec] + [any_spec] * 5 + [vmem_spec], out_specs=(any_spec,) * 3,
                 scratch_shapes=[pltpu.VMEM((n_heads // TILE_HEADS, 4, n_tok, TILE_HEADS, head_dim), bf16), pltpu.VMEM(q_loc.shape, bf16)]
                 + [pltpu.VMEM(pair_shape, bf16)] * 3 + [pltpu.VMEM((5,) + pair_shape, bf16)]
                 + [pltpu.VMEM((2 * n_heads, n_tok), f32), pltpu.VMEM((REACH, 2 * n_heads, n_tok), f32), pltpu.VMEM((8, n_tok), jnp.int32)]
-                + [pltpu.VMEM((3, TILE_HEADS, n_tok, head_dim), bf16)] + [pltpu.VMEM((n_tok, head_dim), f32)] * 3
-                + [dma((n_heads // TILE_HEADS, ROW_PARTS, 4)), dma, dma((n_heads // TILE_HEADS, 3)), dma((REACH,)), dma((REACH,)), dma((n_heads,)), dma((n_heads,))]
-                + [dma((n_heads, ROW_PARTS))] * 8,
+                + [pltpu.VMEM((IN_FLIGHT, 3, n_tok, head_dim), bf16)] + [pltpu.VMEM((IN_FLIGHT, n_tok, head_dim), f32)] * 3
+                + [dma((n_heads // TILE_HEADS, ROW_PARTS, 4)), dma, dma((IN_FLIGHT, 3)), dma((REACH,)), dma((REACH,)), dma((n_heads,)), dma((n_heads,))]
+                + [dma((n_heads, ROW_PARTS))] * 4 + [dma((n_heads,))] * 4,
                 compiler_params=pltpu.CompilerParams(collective_id=0, has_side_effects=True), name="near_grads",
             )(cu_seqlens, q_loc, k_loc, v_loc, o_loc, do_loc, lse_loc.T)
-
-        chip_pos = jnp.arange(1, n_dev // 2 - 1, dtype=jnp.int32)[:, None] * 2 * n_tok
-        cuts = (cu_seqlens[None] >= chip_pos) & (cu_seqlens[None] <= chip_pos + 2 * n_tok)
-        far = jnp.logical_not(jnp.all(jnp.any(cuts, axis=1)))
-        return lax.cond(far, wide, near, q_loc, k_loc, v_loc, o_loc, do_loc, lse_loc, cu_seqlens)
+            rows = n_tok // OUT_STEPS
+            return pl.pallas_call(
+                token_major_kernel, grid=(OUT_STEPS,), out_shape=(jax.ShapeDtypeStruct(q_loc.shape, bf16),) * 3,
+                in_specs=[pl.BlockSpec((n_heads, rows, head_dim), lambda i: (0, i, 0))] * 3,
+                out_specs=[pl.BlockSpec((rows, n_heads, head_dim), lambda i: (i, 0, 0))] * 3, name="token_major", compiler_params=pltpu.CompilerParams(vmem_limit_bytes=67043328))(*heads_out)
+
+        def branch_kernel(cu_ref, out_ref):
+            first = 2 * n_tok
+
+            def scan(n, seen):
+                here = cu_ref[n]
+                return tuple(jnp.where((here >= c * first) & (here <= (c + 1) * first), 1, flag) for c, flag in zip((1, 2), seen))
+
+            seen = lax.fori_loop(0, cu_ref.shape[0], scan, (0, 0), unroll=True)
+            out_ref[0] = 1 - seen[0] * seen[1]
+
+        pick = pl.pallas_call(branch_kernel, out_shape=jax.ShapeDtypeStruct((1,), jnp.int32), in_specs=[smem_spec], out_specs=smem_spec, name="pick_branch")(cu_seqlens)[0]
+        return lax.switch(pick, (near, wide), q_loc, k_loc, v_loc, o_loc, do_loc, lse_loc, cu_seqlens)
 
     return jax.shard_map(device_fn, mesh=mesh, in_specs=(head_spec, head_spec, head_spec, head_spec, head_spec, row_spec, P()), out_specs=(head_spec, head_spec, head_spec), check_vma=False)

time: 121 us -> 117 us (0.967)
  local copies, waits for them, and re-layouts: 6.01 us -> 0 us
  Pallas kernels: 111 us -> 115 us
  other arithmetic: 1.49 us -> 0 us
    pallas_call x0 -> x2, Pallas kernels: none -> 6.14 us  [the longest x1 4.79 us: near(): pl.pallas_call(token_major_kernel, grid=(OUT_STEPS,), out_shape=(jax.Shap...]
    unnamed x7 -> x0, local copies, waits for them, and re-layouts: 6.01 us -> none
    pallas_call x1, Pallas kernels: 111 us -> 109 us  [near(): pl.pallas_call(functools.partial(near_kernel, n_dev, score_scale), out_sh...]
where the time goes in v3:
time: 117 us
  Pallas kernels  115 us (98%)
  between operations  1.29 us (1%)
    pallas_call x1, Pallas kernels, near(): pl.pallas_call(functools.partial(near_kernel, n_dev, score_scale), out_sh...  109 us
    pallas_call x1, Pallas kernels, near(): pl.pallas_call(token_major_kernel, grid=(OUT_STEPS,), out_shape=(jax.Shap...  4.79 us

profile of v3, /device:TPU:3, one launch (start us, length us, event | category | flops | bytes accessed | tf_op | source)
XLA Modules:
  0.0 116.6 jit_solution(17289187479910416530)
XLA Ops:
  0.6 1.3 %pick_branch.1 = s32[1]{0:T(128)} custom-call(s32[67]{0:T(128)} %cu_ref.1), custom_call_target="tpu_custom_call" | custom-call | tf_op jit(solution)/shard_map/pick_branch/pallas_call | solution.py:440
  2.6 113.9 %conditional.1 = ((bf16[256,16,256]{2,1,0:T(8,128)(2,1)}, bf16[256,16,256]{2,1,0:T(8,128)(2,1)}, bf16[256,16,256]{2,1,0:T(8,128)(2,1)})) conditional(s32[]{:T(128)} %bitcast.16, (f32[256,16]{0,1:T(8,128)}, s32[67]{0:T(128)}, bf16[256,16,256]{2,1,0:T(8,128)(2,1)}, bf16[256,16,256]{2,1,0:T(8,128)(2,1)}, bf16[256,16,256]{2,1,0:T(8,128)(2,1)}, ...), branch_computations={%region_0.0_spmd, %region_1.3_spmd} | conditional | flops 17219584 | bytes 105195208 | solution.py:441
  2.6 109.1 %near_grads.1 = (bf16[16,256,256]{2,1,0:T(8,128)(2,1)}, bf16[16,256,256]{2,1,0:T(8,128)(2,1)}, bf16[16,256,256]{2,1,0:T(8,128)(2,1)}) custom-call(s32[67]{0:T(128)} %get-tuple-element.28.cu_ref, bf16[256,16,256]{2,1,0:T(8,128)(2,1)} %get-tuple-element.29.q_ref, bf16[256,16,256]{2,1,0:T(8,128)(2,1)} %get-tuple-element.30.k_ref, ...), custom_call_target="tpu_custom_call" | custom-call | tf_op jit(solution)/shard_map/cond/branch_0_fun/near_grads/pallas_call | solution.py:412
  111.8 4.8 %token_major.1 = (bf16[256,16,256]{2,1,0:T(8,128)(2,1)}, bf16[256,16,256]{2,1,0:T(8,128)(2,1)}, bf16[256,16,256]{2,1,0:T(8,128)(2,1)}) custom-call(bf16[16,256,256]{2,1,0:T(8,128)(2,1)} %get-tuple-element.35.dq_ref, bf16[16,256,256]{2,1,0:T(8,128)(2,1)} %get-tuple-element.36.dk_ref, bf16[16,256,256]{2,1,0:T(8,128)(2,1)} %get-tuple-element.37.dv_ref), custom_call_target="tpu_custom_call" | custom-call | tf_op jit(solution)/shard_map/cond/branch_0_fun/token_major/pallas_call | solution.py:425

commit v4 on v3

--- a/solution.py
+++ b/solution.py
@@ -124,8 +124,8 @@
 
 
 def near_kernel(n_dev, score_scale, cu_ref, q_ref, k_ref, v_ref, o_ref, do_ref, lse_ref, dq_ref, dk_ref, dv_ref,
-                raw, raw_o, qd, kv, pk, win, stat, swin, starts, out_buf, dq_acc, dk_acc, dv_acc,
-                ld_sem, o_sem, out_sem, st_s, st_r, own_s, own_r, x_s, x_r, y_s, y_r, fx_s, fx_r, fy_s, fy_r):
+                raw, raw_o, qd, kv, pk, win, stat, swin, starts, dq_acc, dk_acc, dv_acc,
+                ld_sem, o_sem, st_s, st_r, own_s, own_r, x_s, x_r, y_s, y_r, fx_s, fx_r, fy_s, fy_r):
     me = lax.axis_index("cp")
     core = lax.rem(me, 2)
     chip = me // 2
@@ -296,22 +296,11 @@
         fy_copy(h).wait_recv()
         far_part(h, chip_odd == 0)
 
-    def out_copy(h, which):
-        dst = (dq_ref, dk_ref, dv_ref)[which]
-        return pltpu.make_async_copy(out_buf.at[h % IN_FLIGHT, which], dst.at[h], out_sem.at[h % IN_FLIGHT, which])
-
     def finish(h):
-        @pl.when(h >= IN_FLIGHT)
-        def _():
-            for which in range(3):
-                out_copy(h - IN_FLIGHT, which).wait()
-
         at = h % IN_FLIGHT
-        out_buf[at, 0] = (dq_acc[at] * score_scale).astype(out_buf.dtype)
-        out_buf[at, 1] = (dk_acc[at] * score_scale).astype(out_buf.dtype)
-        out_buf[at, 2] = dv_acc[at].astype(out_buf.dtype)
-        for which in range(3):
-            out_copy(h, which).start()
+        dq_ref[h] = (dq_acc[at] * score_scale).astype(dq_ref.dtype)
+        dk_ref[h] = (dk_acc[at] * score_scale).astype(dk_ref.dtype)
+        dv_ref[h] = dv_acc[at].astype(dv_ref.dtype)
 
     for dist, copy in stats:
         pl.when(me + dist < n_dev)(copy.wait_recv)
@@ -341,14 +330,19 @@
     lax.fori_loop(0, n_heads, drain, 0)
     for dist, copy in stats:
         pl.when(me >= dist)(copy.wait_send)
-    for h in range(n_heads - IN_FLIGHT, n_heads):
-        for which in range(3):
-            out_copy(h, which).wait()
-
-
-def token_major_kernel(dq_ref, dk_ref, dv_ref, dq_out, dk_out, dv_out):
-    for src, dst in ((dq_ref, dq_out), (dk_ref, dk_out), (dv_ref, dv_out)):
-        dst[...] = jnp.swapaxes(src[...], 0, 1)
+
+
+def token_major_kernel(dq_ref, dk_ref, dv_ref, dq_out, dk_out, dv_out, rows_buf, out_sem):
+    part = dq_ref.shape[1] // OUT_STEPS
+    copies = []
+    for r in range(OUT_STEPS):
+        for which, (src, dst) in enumerate(((dq_ref, dq_out), (dk_ref, dk_out), (dv_ref, dv_out))):
+            rows = pl.ds(r * part, part)
+            rows_buf[which, rows] = jnp.swapaxes(src[:, rows], 0, 1)
+            copies.append(pltpu.make_async_copy(rows_buf.at[which, rows], dst.at[rows], out_sem.at[which, r]))
+            copies[-1].start()
+    for copy in copies:
+        copy.wait()
 
 
 def solution(mesh):
@@ -407,25 +401,24 @@
             return tuple(back[n].transpose(1, 0, 2) for n in range(3))
 
         def near(q_loc, k_loc, v_loc, o_loc, do_loc, lse_loc, cu_seqlens):
-            out_one = jax.ShapeDtypeStruct((n_heads, n_tok, head_dim), q_loc.dtype)
+            out_one = pltpu.VMEM((n_heads, n_tok, head_dim), q_loc.dtype)
             bf16, f32 = jnp.bfloat16, jnp.float32
             heads_out = pl.pallas_call(
                 functools.partial(near_kernel, n_dev, score_scale),
                 out_shape=(out_one, out_one, out_one),
-                in_specs=[smem_spec] + [any_spec] * 5 + [vmem_spec], out_specs=(any_spec,) * 3,
+                in_specs=[smem_spec] + [any_spec] * 5 + [vmem_spec], out_specs=(vmem_spec,) * 3,
                 scratch_shapes=[pltpu.VMEM((n_heads // TILE_HEADS, 4, n_tok, TILE_HEADS, head_dim), bf16), pltpu.VMEM(q_loc.shape, bf16)]
                 + [pltpu.VMEM(pair_shape, bf16)] * 3 + [pltpu.VMEM((5,) + pair_shape, bf16)]
                 + [pltpu.VMEM((2 * n_heads, n_tok), f32), pltpu.VMEM((REACH, 2 * n_heads, n_tok), f32), pltpu.VMEM((8, n_tok), jnp.int32)]
-                + [pltpu.VMEM((IN_FLIGHT, 3, n_tok, head_dim), bf16)] + [pltpu.VMEM((IN_FLIGHT, n_tok, head_dim), f32)] * 3
-                + [dma((n_heads // TILE_HEADS, ROW_PARTS, 4)), dma, dma((IN_FLIGHT, 3)), dma((REACH,)), dma((REACH,)), dma((n_heads,)), dma((n_heads,))]
+                + [pltpu.VMEM((IN_FLIGHT, n_tok, head_dim), f32)] * 3
+                + [dma((n_heads // TILE_HEADS, ROW_PARTS, 4)), dma, dma((REACH,)), dma((REACH,)), dma((n_heads,)), dma((n_heads,))]
                 + [dma((n_heads, ROW_PARTS))] * 4 + [dma((n_heads,))] * 4,
-                compiler_params=pltpu.CompilerParams(collective_id=0, has_side_effects=True), name="near_grads",
+                compiler_params=pltpu.CompilerParams(collective_id=0, has_side_effects=True, vmem_limit_bytes=50 * 1024 * 1024), name="near_grads",
             )(cu_seqlens, q_loc, k_loc, v_loc, o_loc, do_loc, lse_loc.T)
-            rows = n_tok // OUT_STEPS
             return pl.pallas_call(
-                token_major_kernel, grid=(OUT_STEPS,), out_shape=(jax.ShapeDtypeStruct(q_loc.shape, bf16),) * 3,
-                in_specs=[pl.BlockSpec((n_heads, rows, head_dim), lambda i: (0, i, 0))] * 3,
-                out_specs=[pl.BlockSpec((rows, n_heads, head_dim), lambda i: (i, 0, 0))] * 3, name="token_major", compiler_params=pltpu.CompilerParams(vmem_limit_bytes=67043328))(*heads_out)
+                token_major_kernel, out_shape=(pltpu.HBM(q_loc.shape, bf16),) * 3, in_specs=[vmem_spec] * 3, out_specs=(any_spec,) * 3,
+                scratch_shapes=[pltpu.VMEM((3,) + q_loc.shape, bf16), dma((3, OUT_STEPS))],
+                name="token_major", compiler_params=pltpu.CompilerParams(vmem_limit_bytes=20 * 1024 * 1024))(*heads_out)
 
         def branch_kernel(cu_ref, out_ref):
             first = 2 * n_tok

time: 117 us -> 115 us (0.983)
  Pallas kernels: 115 us -> 113 us
    pallas_call x1, Pallas kernels: 4.79 us -> 2.96 us  [near(): pl.pallas_call(token_major_kernel, out_shape=(pltpu.HBM(q_loc.shape, bf16...]
where the time goes in v4:
time: 115 us
  Pallas kernels  113 us (98%)
  between operations  1.47 us (1%)
    pallas_call x1, Pallas kernels, near(): pl.pallas_call(functools.partial(near_kernel, n_dev, score_scale), out_sh...  109 us
    pallas_call x1, Pallas kernels, near(): pl.pallas_call(token_major_kernel, out_shape=(pltpu.HBM(q_loc.shape, bf16...  2.96 us

profile of v4, /device:TPU:3, one launch (start us, length us, event | category | flops | bytes accessed | tf_op | source)
XLA Modules:
  0.0 114.6 jit_solution(4859587544022970023)
XLA Ops:
  0.6 1.3 %pick_branch.1 = s32[1]{0:T(128)} custom-call(s32[67]{0:T(128)} %cu_ref.1), custom_call_target="tpu_custom_call" | custom-call | tf_op jit(solution)/shard_map/pick_branch/pallas_call | solution.py:433
  2.6 111.8 %conditional.1 = ((bf16[256,16,256]{2,1,0:T(8,128)(2,1)}, bf16[256,16,256]{2,1,0:T(8,128)(2,1)}, bf16[256,16,256]{2,1,0:T(8,128)(2,1)})) conditional(s32[]{:T(128)} %bitcast.16, (f32[256,16]{0,1:T(8,128)}, s32[67]{0:T(128)}, bf16[256,16,256]{2,1,0:T(8,128)(2,1)}, bf16[256,16,256]{2,1,0:T(8,128)(2,1)}, bf16[256,16,256]{2,1,0:T(8,128)(2,1)}, ...), branch_computations={%region_0.0_spmd, %region_1.3_spmd} | conditional | flops 17219584 | bytes 105195208 | solution.py:434
  2.6 108.5 %near_grads.1 = (bf16[16,256,256]{2,1,0:T(8,128)(2,1)S(1)}, bf16[16,256,256]{2,1,0:T(8,128)(2,1)S(1)}, bf16[16,256,256]{2,1,0:T(8,128)(2,1)S(1)}) custom-call(s32[67]{0:T(128)} %get-tuple-element.28.cu_ref, bf16[256,16,256]{2,1,0:T(8,128)(2,1)} %get-tuple-element.29.q_ref, bf16[256,16,256]{2,1,0:T(8,128)(2,1)} %get-tuple-element.30.k_ref, ...), custom_call_target="tpu_custom_call" | custom-call | tf_op jit(solution)/shard_map/cond/branch_0_fun/near_grads/pallas_call | solution.py:406
  111.2 3.0 %token_major.1 = (bf16[256,16,256]{2,1,0:T(8,128)(2,1)}, bf16[256,16,256]{2,1,0:T(8,128)(2,1)}, bf16[256,16,256]{2,1,0:T(8,128)(2,1)}) custom-call(bf16[16,256,256]{2,1,0:T(8,128)(2,1)S(1)} %get-tuple-element.35.dq_ref, bf16[16,256,256]{2,1,0:T(8,128)(2,1)S(1)} %get-tuple-element.36.dk_ref, bf16[16,256,256]{2,1,0:T(8,128)(2,1)S(1)} %get-tuple-element.37.dv_ref), custom_call_target="tpu_custom_call" | custom-call | tf_op jit(solution)/shard_map/cond/branch_0_fun/token_major/pallas_call | solution.py:418

commit v5 on v4

--- a/solution.py
+++ b/solution.py
@@ -84,6 +84,16 @@
     for mask in order:
         for copy in copies(mask):
             copy.wait()
+
+
+def turn_kernel(*refs):
+    n_out = len(refs) // 2 if len(refs) % 2 == 0 else 1
+    srcs, dsts = refs[:len(refs) - n_out], refs[len(refs) - n_out:]
+    for n, src in enumerate(srcs):
+        if n_out == 1:
+            dsts[0][n] = jnp.swapaxes(src[...], 0, 1)
+        else:
+            dsts[n][...] = jnp.swapaxes(src[0], 0, 1)
 
 
 def head_kernel(score_scale, start_ref, got_ref, gstat_ref, rows_ref, out_ref, dq_acc, dk_acc, dv_acc):
@@ -174,8 +184,11 @@
         rows, heads = pl.ds(r * part, part), pl.ds(half * TILE_HEADS, TILE_HEADS)
         return pltpu.make_async_copy(src.at[rows, heads], raw.at[half, which, rows], ld_sem.at[half, r, which])
 
+    for half, r in units[:1]:
+        for which in range(4):
+            load(half, r, which).start()
     greet_all(n_dev, me)
-    for half, r in units:
+    for half, r in units[1:]:
         for which in range(4):
             load(half, r, which).start()
     load_o = pltpu.make_async_copy(o_ref, raw_o, o_sem)
@@ -368,7 +381,10 @@
             delta_loc = jnp.einsum("shd,shd->hs", do_loc, o_loc, preferred_element_type=f32)
             parts = [item.reshape(n_dev, per, n_tok) for item in (lse_loc.T, delta_loc)]
             stat = jnp.concatenate(parts + [jnp.zeros((n_dev, 8 - 2 * per, n_tok), f32)], axis=1)
-            ops = jnp.stack([q_loc, k_loc, v_loc, do_loc]).transpose(0, 2, 1, 3)
+            rows = n_tok // OUT_STEPS
+            row_blk = pl.BlockSpec((rows, n_heads, head_dim), lambda i: (i, 0, 0))
+            ops = pl.pallas_call(turn_kernel, grid=(OUT_STEPS,), out_shape=jax.ShapeDtypeStruct((4, n_heads, n_tok, head_dim), bf16), in_specs=[row_blk] * 4,
+                                 out_specs=pl.BlockSpec((4, n_heads, rows, head_dim), lambda i: (0, 0, i, 0)), name="turn_in")(q_loc, k_loc, v_loc, do_loc)
 
             def heads_of(dev):
                 return pl.ds(dev * per, per)
@@ -398,7 +414,8 @@
                 out_shape=jax.ShapeDtypeStruct((n_dev, 3, per, n_tok, head_dim), bf16), name="head_grads",
             )(start_rows[:, 0], got, gstat, start_rows)
             back, = call(out_pairs, 1, 2, (jax.ShapeDtypeStruct((3, n_heads, n_tok, head_dim), bf16),), grads)
-            return tuple(back[n].transpose(1, 0, 2) for n in range(3))
+            head_blks = [pl.BlockSpec((1, n_heads, rows, head_dim), lambda i, n=n: (n, 0, i, 0)) for n in range(3)]
+            return pl.pallas_call(turn_kernel, grid=(OUT_STEPS,), out_shape=(pltpu.HBM(q_loc.shape, bf16),) * 3, in_specs=head_blks, out_specs=[row_blk] * 3, name="turn_out")(back, back, back)
 
         def near(q_loc, k_loc, v_loc, o_loc, do_loc, lse_loc, cu_seqlens):
             out_one = pltpu.VMEM((n_heads, n_tok, head_dim), q_loc.dtype)

time: 115 us -> 115 us (level)
  no operation moved by 1% of the time
where the time goes in v5:
time: 115 us; the launch traced here: 114 us
  Pallas kernels  113 us (98%)
  between operations  1.45 us (1%)
    pallas_call x1, Pallas kernels, near(): pl.pallas_call(functools.partial(near_kernel, n_dev, score_scale), out_sh...  108 us
    pallas_call x1, Pallas kernels, near(): pl.pallas_call(token_major_kernel, out_shape=(pltpu.HBM(q_loc.shape, bf16...  2.96 us

profile of v5, /device:TPU:3, one launch (start us, length us, event | category | flops | bytes accessed | tf_op | source)
XLA Modules:
  0.0 114.4 jit_solution(4631912907116905820)
XLA Ops:
  0.6 1.3 %pick_branch.1 = s32[1]{0:T(128)} custom-call(s32[67]{0:T(128)} %cu_ref.1), custom_call_target="tpu_custom_call" | custom-call | tf_op jit(solution)/shard_map/pick_branch/pallas_call | solution.py:450
  2.6 111.6 %conditional.1 = ((bf16[256,16,256]{2,1,0:T(8,128)(2,1)}, bf16[256,16,256]{2,1,0:T(8,128)(2,1)}, bf16[256,16,256]{2,1,0:T(8,128)(2,1)})) conditional(s32[]{:T(128)} %bitcast.4, (f32[256,16]{0,1:T(8,128)}, s32[67]{0:T(128)}, bf16[256,16,256]{2,1,0:T(8,128)(2,1)}, bf16[256,16,256]{2,1,0:T(8,128)(2,1)}, bf16[256,16,256]{2,1,0:T(8,128)(2,1)}, ...), branch_computations={%region_0.0_spmd, %region_1.3_spmd} | conditional | flops 4636672 | bytes 12920412 | solution.py:451
  2.6 108.5 %near_grads.1 = (bf16[16,256,256]{2,1,0:T(8,128)(2,1)S(1)}, bf16[16,256,256]{2,1,0:T(8,128)(2,1)S(1)}, bf16[16,256,256]{2,1,0:T(8,128)(2,1)S(1)}) custom-call(s32[67]{0:T(128)} %get-tuple-element.28.cu_ref, bf16[256,16,256]{2,1,0:T(8,128)(2,1)} %get-tuple-element.29.q_ref, bf16[256,16,256]{2,1,0:T(8,128)(2,1)} %get-tuple-element.30.k_ref, ...), custom_call_target="tpu_custom_call" | custom-call | tf_op jit(solution)/shard_map/cond/branch_0_fun/near_grads/pallas_call | solution.py:423
  111.1 3.0 %token_major.1 = (bf16[256,16,256]{2,1,0:T(8,128)(2,1)}, bf16[256,16,256]{2,1,0:T(8,128)(2,1)}, bf16[256,16,256]{2,1,0:T(8,128)(2,1)}) custom-call(bf16[16,256,256]{2,1,0:T(8,128)(2,1)S(1)} %get-tuple-element.35.dq_ref, bf16[16,256,256]{2,1,0:T(8,128)(2,1)S(1)} %get-tuple-element.36.dk_ref, bf16[16,256,256]{2,1,0:T(8,128)(2,1)S(1)} %get-tuple-element.37.dv_ref), custom_call_target="tpu_custom_call" | custom-call | tf_op jit(solution)/shard_map/cond/branch_0_fun/token_major/pallas_call | solution.py:435

commit v6 on v5

--- a/solution.py
+++ b/solution.py
@@ -297,17 +297,18 @@
         pl.when(core == 1)(lambda: key_blocks(h, [0]))
         pl.when(core == 0)(lambda: query_blocks(h, [4]))
 
-    def far_part(h, keys):
-        pl.when(keys)(lambda: key_blocks(h, [1, 2 * core]))
-        pl.when(jnp.logical_not(keys))(lambda: query_blocks(h, [3, 2 + 2 * core]))
+    def far_part(h, keys, key_slots, query_slots):
+        pl.when(keys)(lambda: key_blocks(h, key_slots))
+        pl.when(jnp.logical_not(keys))(lambda: query_blocks(h, query_slots))
 
     def x_part(h):
         fx_copy(h).wait_recv()
-        far_part(h, chip_odd == 1)
+        far_part(h, chip_odd == 1, [1, 2 * core], [3, 2 + 2 * core])
 
     def y_part(h):
+        far_part(h, chip_odd == 0, [1], [3])
         fy_copy(h).wait_recv()
-        far_part(h, chip_odd == 0)
+        far_part(h, chip_odd == 0, [2 * core], [2 + 2 * core])
 
     def finish(h):
         at = h % IN_FLIGHT

time: 115 us -> 114 us (level)
  no operation moved by 1% of the time
where the time goes in v6:
time: 114 us
  Pallas kernels  113 us (99%)
  between operations  1.45 us (1%)
    pallas_call x1, Pallas kernels, near(): pl.pallas_call(functools.partial(near_kernel, n_dev, score_scale), out_sh...  108 us
    pallas_call x1, Pallas kernels, near(): pl.pallas_call(token_major_kernel, out_shape=(pltpu.HBM(q_loc.shape, bf16...  2.96 us

profile of v6, /device:TPU:3, one launch (start us, length us, event | category | flops | bytes accessed | tf_op | source)
XLA Modules:
  0.0 114.2 jit_solution(8585735054896548915)
XLA Ops:
  0.6 1.3 %pick_branch.1 = s32[1]{0:T(128)} custom-call(s32[67]{0:T(128)} %cu_ref.1), custom_call_target="tpu_custom_call" | custom-call | tf_op jit(solution)/shard_map/pick_branch/pallas_call | solution.py:451
  2.6 111.5 %conditional.1 = ((bf16[256,16,256]{2,1,0:T(8,128)(2,1)}, bf16[256,16,256]{2,1,0:T(8,128)(2,1)}, bf16[256,16,256]{2,1,0:T(8,128)(2,1)})) conditional(s32[]{:T(128)} %bitcast.4, (f32[256,16]{0,1:T(8,128)}, s32[67]{0:T(128)}, bf16[256,16,256]{2,1,0:T(8,128)(2,1)}, bf16[256,16,256]{2,1,0:T(8,128)(2,1)}, bf16[256,16,256]{2,1,0:T(8,128)(2,1)}, ...), branch_computations={%region_0.0_spmd, %region_1.3_spmd} | conditional | flops 4636672 | bytes 12920412 | solution.py:452
  2.6 108.3 %near_grads.1 = (bf16[16,256,256]{2,1,0:T(8,128)(2,1)S(1)}, bf16[16,256,256]{2,1,0:T(8,128)(2,1)S(1)}, bf16[16,256,256]{2,1,0:T(8,128)(2,1)S(1)}) custom-call(s32[67]{0:T(128)} %get-tuple-element.28.cu_ref, bf16[256,16,256]{2,1,0:T(8,128)(2,1)} %get-tuple-element.29.q_ref, bf16[256,16,256]{2,1,0:T(8,128)(2,1)} %get-tuple-element.30.k_ref, ...), custom_call_target="tpu_custom_call" | custom-call | tf_op jit(solution)/shard_map/cond/branch_0_fun/near_grads/pallas_call | solution.py:424
  110.9 3.0 %token_major.1 = (bf16[256,16,256]{2,1,0:T(8,128)(2,1)}, bf16[256,16,256]{2,1,0:T(8,128)(2,1)}, bf16[256,16,256]{2,1,0:T(8,128)(2,1)}) custom-call(bf16[16,256,256]{2,1,0:T(8,128)(2,1)S(1)} %get-tuple-element.35.dq_ref, bf16[16,256,256]{2,1,0:T(8,128)(2,1)S(1)} %get-tuple-element.36.dk_ref, bf16[16,256,256]{2,1,0:T(8,128)(2,1)S(1)} %get-tuple-element.37.dv_ref), custom_call_target="tpu_custom_call" | custom-call | tf_op jit(solution)/shard_map/cond/branch_0_fun/token_major/pallas_call | solution.py:436

commit v7 on v6

--- a/solution.py
+++ b/solution.py
@@ -12,6 +12,7 @@
 ROW_PARTS = 2
 IN_FLIGHT = 4
 OUT_STEPS = 2
+OUT_PIECES = 4
 LOG2E = 1.4426950408889634
 MESH_ID = pl.DeviceIdType.MESH
 
@@ -347,9 +348,9 @@
 
 
 def token_major_kernel(dq_ref, dk_ref, dv_ref, dq_out, dk_out, dv_out, rows_buf, out_sem):
-    part = dq_ref.shape[1] // OUT_STEPS
+    part = dq_ref.shape[1] // OUT_PIECES
     copies = []
-    for r in range(OUT_STEPS):
+    for r in range(OUT_PIECES):
         for which, (src, dst) in enumerate(((dq_ref, dq_out), (dk_ref, dk_out), (dv_ref, dv_out))):
             rows = pl.ds(r * part, part)
             rows_buf[which, rows] = jnp.swapaxes(src[:, rows], 0, 1)
@@ -435,7 +436,7 @@
             )(cu_seqlens, q_loc, k_loc, v_loc, o_loc, do_loc, lse_loc.T)
             return pl.pallas_call(
                 token_major_kernel, out_shape=(pltpu.HBM(q_loc.shape, bf16),) * 3, in_specs=[vmem_spec] * 3, out_specs=(any_spec,) * 3,
-                scratch_shapes=[pltpu.VMEM((3,) + q_loc.shape, bf16), dma((3, OUT_STEPS))],
+                scratch_shapes=[pltpu.VMEM((3,) + q_loc.shape, bf16), dma((3, OUT_PIECES))],
                 name="token_major", compiler_params=pltpu.CompilerParams(vmem_limit_bytes=20 * 1024 * 1024))(*heads_out)
 
         def branch_kernel(cu_ref, out_ref):

time: 114 us -> 114 us (level)
  no operation moved by 1% of the time
where the time goes in v7:
time: 114 us
  Pallas kernels  113 us (99%)
  between operations  1.45 us (1%)
    pallas_call x1, Pallas kernels, near(): pl.pallas_call(functools.partial(near_kernel, n_dev, score_scale), out_sh...  108 us
    pallas_call x1, Pallas kernels, near(): pl.pallas_call(token_major_kernel, out_shape=(pltpu.HBM(q_loc.shape, bf16...  2.88 us

profile of v7, /device:TPU:3, one launch (start us, length us, event | category | flops | bytes accessed | tf_op | source)
XLA Modules:
  0.0 114.2 jit_solution(13848883856163927159)
XLA Ops:
  0.6 1.3 %pick_branch.1 = s32[1]{0:T(128)} custom-call(s32[67]{0:T(128)} %cu_ref.1), custom_call_target="tpu_custom_call" | custom-call | tf_op jit(solution)/shard_map/pick_branch/pallas_call | solution.py:452
  2.6 111.4 %conditional.1 = ((bf16[256,16,256]{2,1,0:T(8,128)(2,1)}, bf16[256,16,256]{2,1,0:T(8,128)(2,1)}, bf16[256,16,256]{2,1,0:T(8,128)(2,1)})) conditional(s32[]{:T(128)} %bitcast.4, (f32[256,16]{0,1:T(8,128)}, s32[67]{0:T(128)}, bf16[256,16,256]{2,1,0:T(8,128)(2,1)}, bf16[256,16,256]{2,1,0:T(8,128)(2,1)}, bf16[256,16,256]{2,1,0:T(8,128)(2,1)}, ...), branch_computations={%region_0.0_spmd, %region_1.3_spmd} | conditional | flops 4636672 | bytes 12920412 | solution.py:453
  2.6 108.3 %near_grads.1 = (bf16[16,256,256]{2,1,0:T(8,128)(2,1)S(1)}, bf16[16,256,256]{2,1,0:T(8,128)(2,1)S(1)}, bf16[16,256,256]{2,1,0:T(8,128)(2,1)S(1)}) custom-call(s32[67]{0:T(128)} %get-tuple-element.28.cu_ref, bf16[256,16,256]{2,1,0:T(8,128)(2,1)} %get-tuple-element.29.q_ref, bf16[256,16,256]{2,1,0:T(8,128)(2,1)} %get-tuple-element.30.k_ref, ...), custom_call_target="tpu_custom_call" | custom-call | tf_op jit(solution)/shard_map/cond/branch_0_fun/near_grads/pallas_call | solution.py:425
  110.9 2.9 %token_major.1 = (bf16[256,16,256]{2,1,0:T(8,128)(2,1)}, bf16[256,16,256]{2,1,0:T(8,128)(2,1)}, bf16[256,16,256]{2,1,0:T(8,128)(2,1)}) custom-call(bf16[16,256,256]{2,1,0:T(8,128)(2,1)S(1)} %get-tuple-element.35.dq_ref, bf16[16,256,256]{2,1,0:T(8,128)(2,1)S(1)} %get-tuple-element.36.dk_ref, bf16[16,256,256]{2,1,0:T(8,128)(2,1)S(1)} %get-tuple-element.37.dv_ref), custom_call_target="tpu_custom_call" | custom-call | tf_op jit(solution)/shard_map/cond/branch_0_fun/token_major/pallas_call | solution.py:437
